TPU v7x, 256 devices: a whole 4x4x8 slice. The times are simulated.
256 devices in a mesh: gx: 8 (over x, core), gy: 8 (over z), gz: 4 (over y).
Axes of the slice: x: 4, y: 4, z: 8, core: 2. Of those that a mesh axis runs over, the one named last changes fastest.
Arguments:
- particle_mass: float32 [8388608], P(('gx', 'gy', 'gz')), may hold values from 0.5 to 2
- particle_velocity: float32 [3, 8388608], P(None, ('gx', 'gy', 'gz')), may hold values from -6 to 6
- particle_affine: float32 [9, 8388608], P(None, ('gx', 'gy', 'gz')), may hold values from -6 to 6
- particle_cell: int32 [3, 8388608], P(None, ('gx', 'gy', 'gz')), may hold values from 0 to 13
- particle_fraction: int32 [3, 8388608], P(None, ('gx', 'gy', 'gz')), may hold values from 0 to 1023
- block_owner: int32 [16384, 1], P(('gx', 'gy', 'gz')), may hold values from 0 to 31; in each aligned block of 64 rows (0 to 63, 64 to 127, ...) at most 4 rows name the same one
- block_slot: int32 [16384], P(('gx', 'gy', 'gz')), may hold values from 0 to 15
- block_count: int32 [16384], P(('gx', 'gy', 'gz')), may hold values from 128 to 512
- cell_drag: float32 [4096, 4096], P(('gx', 'gy', 'gz')), may hold values from 0.5 to 2
Outputs:
- grid_velocity: float32 [4096, 3, 4096], P(('gx', 'gy', 'gz'))
- new_velocity: float32 [3, 8388608], P(None, ('gx', 'gy', 'gz'))
- new_affine: float32 [9, 8388608], P(None, ('gx', 'gy', 'gz'))
Inputs may be any that keep to these rules, and one draw needn't show every extreme that they name: `block_owner`: owner index counted over the devices with the particle device's own gx index, in gy+gz order; among the rows of one device, no owner is named more than 4 times. `block_count`: slots at or beyond the count are absent. `particle_cell`: A particle's three stencil nodes lie inside its grid block.
All inputs are finite; a program needn't handle non-finite values.
Results may differ from a plain program's by a relative error of at most 0.0085.
Values may be sent and summed in bfloat16 or wider, within the bound.
A program may use at most 128 MiB of HBM per device.

v0:
```python
import jax
import jax.numpy as jnp
from jax import lax
from jax.sharding import PartitionSpec as P

EDGE = 16
QUANT = 1024


batch_blocks = 4


def spline(offset):
    magnitude = jnp.abs(offset)
    inner_part = 0.75 - magnitude * magnitude
    outer_part = 0.5 * (1.5 - magnitude) * (1.5 - magnitude)
    return jnp.where(magnitude < 0.5, inner_part, jnp.where(magnitude < 1.5, outer_part, 0.0))


def particle_table(
    particle_mass, particle_velocity, particle_affine, particle_cell, particle_fraction, block_count
):
    blocks = block_count.shape[0]
    batch_shape = (blocks, particle_mass.shape[0] // blocks)
    places = jnp.arange(batch_shape[1], dtype=jnp.int32)
    present = places[None, :] < block_count[:, None]
    live_mass = jnp.where(present, particle_mass.reshape(batch_shape), 0.0)
    position = (
        particle_cell.astype(jnp.float32)
        + 0.5
        + (particle_fraction.astype(jnp.float32) + 0.5) / QUANT
    )
    return jnp.concatenate(
        [
            live_mass[None],
            particle_velocity.reshape((3,) + batch_shape),
            particle_affine.reshape((9,) + batch_shape),
            position.reshape((3,) + batch_shape),
        ],
        axis=0,
    )


def stencil(particle_data):
    node_coords = jnp.arange(EDGE, dtype=jnp.float32)
    offset = node_coords[None, :, None, None] - particle_data[13:16][:, None]
    weights = spline(offset)
    return (weights, weights * offset)


def planes(weights, slopes):

    def outer(first_factor, second_factor):
        product_table = first_factor[:, None] * second_factor[None, :]
        return product_table.reshape((EDGE * EDGE,) + product_table.shape[2:]).astype(jnp.bfloat16)

    return (
        outer(weights[1], weights[2]),
        outer(slopes[1], weights[2]),
        outer(weights[1], slopes[2]),
    )


def deposit(particle_data):
    batch_shape = particle_data.shape[1:]
    weights, slopes = stencil(particle_data)
    plane_zero, plane_one, plane_two = planes(weights, slopes)
    live_mass = particle_data[0]
    along_x = weights[0]
    slope_x = slopes[0]
    affine = particle_data[4:13].reshape((3, 3) + batch_shape)
    mass_lead = (live_mass[None] * along_x)[None]
    momentum_lead = live_mass[None, None] * (
        particle_data[1:4][:, None] * along_x[None] + affine[:, 0][:, None] * slope_x[None]
    )
    lead_zero = jnp.concatenate([mass_lead, momentum_lead], axis=0).astype(jnp.bfloat16)
    lead_one = (live_mass[None, None] * affine[:, 1][:, None] * along_x[None]).astype(jnp.bfloat16)
    lead_two = (live_mass[None, None] * affine[:, 2][:, None] * along_x[None]).astype(jnp.bfloat16)

    def contract(lead, plane):
        flattened = lead.reshape((-1,) + batch_shape)
        return jnp.einsum("anp,bnp->nab", flattened, plane, preferred_element_type=jnp.float32)

    count_blocks = batch_shape[0]
    dep_zero = contract(lead_zero, plane_zero).reshape(count_blocks, 4, -1)
    dep_one = contract(lead_one, plane_one).reshape(count_blocks, 3, -1)
    dep_two = contract(lead_two, plane_two).reshape(count_blocks, 3, -1)
    return jnp.concatenate([dep_zero[:, :1], dep_zero[:, 1:] + dep_one + dep_two], axis=1)


def interpolate(particle_data, grid_rows):
    batch_shape = particle_data.shape[1:]
    weights, slopes = stencil(particle_data)
    plane_zero, plane_one, plane_two = planes(weights, slopes)
    along_x = weights[0]
    slope_x = slopes[0]
    flattened = grid_rows.reshape(batch_shape[0], 3 * EDGE, EDGE * EDGE)

    def contract(plane):
        moment = jnp.einsum("nab,bnp->anp", flattened, plane, preferred_element_type=jnp.float32)
        return moment.reshape((3, EDGE) + batch_shape)

    moment_zero = contract(plane_zero)
    moment_one = contract(plane_one)
    moment_two = contract(plane_two)
    velocity_out = jnp.sum(along_x[None] * moment_zero, axis=1)
    column_zero = 4.0 * jnp.sum(slope_x[None] * moment_zero, axis=1)
    column_one = 4.0 * jnp.sum(along_x[None] * moment_one, axis=1)
    column_two = 4.0 * jnp.sum(along_x[None] * moment_two, axis=1)
    affine_out = jnp.stack([column_zero, column_one, column_two], axis=1).reshape(
        (9,) + batch_shape
    )
    present = (particle_data[0] > 0.0).astype(jnp.float32)
    return jnp.concatenate([velocity_out, affine_out], axis=0) * present[None]


def deposit_all(particle_data):
    block_total = particle_data.shape[1]

    def deposit_advance(state_carry, step_index):
        portion = lax.dynamic_slice_in_dim(
            particle_data, step_index * batch_blocks, batch_blocks, 1
        )
        return (state_carry, deposit(portion))

    unused, stacked = lax.scan(
        deposit_advance,
        jnp.zeros((), jnp.float32),
        jnp.arange(block_total // batch_blocks, dtype=jnp.int32),
    )
    return stacked.reshape((block_total,) + stacked.shape[2:])


def interpolate_all(particle_data, grid_rows):
    block_total = particle_data.shape[1]

    def interpolate_advance(step_index, result):
        first_block = step_index * batch_blocks
        portion = lax.dynamic_slice_in_dim(particle_data, first_block, batch_blocks, 1)
        cell_rows = lax.dynamic_slice_in_dim(grid_rows, first_block, batch_blocks, 0)
        return lax.dynamic_update_slice_in_dim(
            result, interpolate(portion, cell_rows), first_block, 1
        )

    initial = jnp.zeros((12, block_total, particle_data.shape[2]), jnp.float32)
    return lax.fori_loop(0, block_total // batch_blocks, interpolate_advance, initial)


def send_slots(owners, group_size, capacity):
    targets = jnp.arange(group_size, dtype=jnp.int32)
    matches = (owners[:, None] == targets[None, :]).astype(jnp.int32)
    earlier = jnp.cumsum(matches, axis=0) - matches
    ranking = jnp.sum(earlier * matches, axis=1)
    return owners * capacity + ranking


def slot_sources(destination, slot_count):
    positions = jnp.arange(slot_count, dtype=jnp.int32)
    matches = destination[None, :] == positions[:, None]
    block_numbers = jnp.arange(destination.shape[0], dtype=jnp.int32)
    source = jnp.sum(jnp.where(matches, block_numbers[None, :], 0), axis=1)
    return (source, jnp.any(matches, axis=1))


def match_tiles(arrived_tiles, tile_count):
    tile_numbers = jnp.arange(tile_count, dtype=jnp.float32)
    return (arrived_tiles[None, :] == tile_numbers[:, None]).astype(jnp.float32)


def update_grid(deposits, tile_match, cell_drag):
    tile_count = tile_match.shape[0]
    flattened = deposits.reshape(deposits.shape[0], -1)
    summed = jnp.dot(tile_match, flattened, preferred_element_type=jnp.float32)
    summed = summed.reshape((tile_count,) + deposits.shape[1:])
    grid_velocity = summed[:, 1:] / (summed[:, :1] + cell_drag[:, None, :])
    rounded = grid_velocity.astype(jnp.bfloat16)
    picked = jnp.dot(
        tile_match.T.astype(jnp.bfloat16),
        rounded.reshape(tile_count, -1),
        preferred_element_type=jnp.float32,
    )
    cell_rows = picked.astype(jnp.bfloat16).reshape((deposits.shape[0], 3, -1))
    return (grid_velocity, cell_rows)


def per_device(
    particle_mass,
    particle_velocity,
    particle_affine,
    particle_cell,
    particle_fraction,
    block_owner,
    block_slot,
    block_count,
    cell_drag,
):
    group_size = lax.axis_size(("gy", "gz"))
    blocks = block_count.shape[0]
    capacity = max(1, 2 * blocks // group_size)
    slot_count = group_size * capacity
    tile_count = cell_drag.shape[0]
    particle_data = particle_table(
        particle_mass,
        particle_velocity,
        particle_affine,
        particle_cell,
        particle_fraction,
        block_count,
    )
    destination = send_slots(block_owner[:, 0], group_size, capacity)
    source, filled = slot_sources(destination, slot_count)
    tile_ids = jnp.where(filled, jnp.take(block_slot, source), -1).astype(jnp.float32)
    deposits = deposit_all(particle_data)
    outgoing = jnp.where(filled[:, None, None], jnp.take(deposits, source, axis=0), 0.0)
    arrived, arrived_tiles = (
        lax.all_to_all(outgoing, ("gy", "gz"), split_axis=0, concat_axis=0, tiled=True),
        lax.all_to_all(tile_ids, ("gy", "gz"), split_axis=0, concat_axis=0, tiled=True),
    )
    tile_match = match_tiles(arrived_tiles, tile_count)
    grid_velocity, cell_rows = update_grid(arrived, tile_match, cell_drag)
    returned = lax.all_to_all(cell_rows, ("gy", "gz"), split_axis=0, concat_axis=0, tiled=True)
    finished = interpolate_all(particle_data, jnp.take(returned, destination, axis=0))
    new_velocity = finished[:3].reshape(3, -1)
    new_affine = finished[3:].reshape(9, -1)
    return (grid_velocity, new_velocity, new_affine)


def solution(mesh):
    return jax.shard_map(
        per_device,
        mesh=mesh,
        in_specs=(
            P(("gx", "gy", "gz")),
            P(None, ("gx", "gy", "gz")),
            P(None, ("gx", "gy", "gz")),
            P(None, ("gx", "gy", "gz")),
            P(None, ("gx", "gy", "gz")),
            P(("gx", "gy", "gz"), None),
            P(("gx", "gy", "gz")),
            P(("gx", "gy", "gz")),
            P(("gx", "gy", "gz"), None),
        ),
        out_specs=(
            P(("gx", "gy", "gz"), None, None),
            P(None, ("gx", "gy", "gz")),
            P(None, ("gx", "gy", "gz")),
        ),
        check_vma=False,
    )
```

profile of v0, /device:TPU:34, one launch (start us, length us, event | category | flops | bytes accessed | tf_op | source)
XLA Modules:
  0.0 569.0 jit_solution(11761494286336790737)
XLA Ops:
  5.7 11.4 %all-to-all-start = ((f32[32,4,1]{1,2,0:T(1,128)}), f32[32,4,1]{1,2,0:T(1,128)S(1)}, u32[]{:S(2)}, u32[]{:S(2)}) async-start(f32[32,4,1]{1,2,0:T(1,128)} %copy.85), calls=%async_computation | async-start | bytes 32768 | tf_op jit(solution)/shard_map/all_to_all | solution.py:217
  17.1 2.8 copy.92
  21.8 1.6 pad_maximum_fusion.2
  23.4 167.7 %while.23 = (s32[]{:T(128)}, bf16[16,4,4,4096]{3,2,1,0:T(4,128)(2,1)}, s32[16]{0:T(128)S(1)}, f32[16,64,512]{2,1,0:T(8,128)}, s32[]{:T(128)}, /*index=5*/s32[]{:...) while((s32[]{:T(128)}, bf16[16,4,4,4096]{3,2,1,0:T(4,128)(2,1)}, s32[16]{0:T(128)S(1)}, ...), condition=%wide.region_5.6_spmd, body=%wide.region_4.5_spmd.sunk | while | flops 173600768 | bytes 15057635 | solution.py:126
  29.9 1.4 fusion.80
  31.4 1.4 fusion.79
  40.4 1.4 fusion.80
  41.9 1.4 fusion.79
  50.9 1.4 fusion.80
  52.4 1.4 fusion.79
  61.4 1.4 fusion.80
  71.9 1.4 fusion.80
  73.3 1.4 fusion.79
  82.3 1.4 fusion.80
  83.8 1.4 fusion.79
  92.8 1.4 fusion.80
  94.3 1.4 fusion.79
  103.3 1.4 fusion.80
  113.8 1.4 fusion.80
  115.3 1.4 fusion.79
  124.3 1.4 fusion.80
  125.7 1.4 fusion.79
  134.7 1.4 fusion.80
  136.2 1.4 fusion.79
  145.2 1.4 fusion.80
  157.2 1.4 fusion.79
  166.2 1.4 fusion.80
  167.7 1.4 fusion.79
  176.7 1.4 fusion.80
  178.1 1.4 fusion.79
  187.2 1.4 fusion.80
  191.1 9.1 %gather_fusion.1 = bf16[128,4,4096]{2,1,0:T(4,128)(2,1)} fusion(bf16[64,4,4096]{2,1,0:T(4,128)(2,1)} %bitcast.212, s32[1024]{0:T(1024)S(1)} %pad_clamp_fusion.1), kind=kCustom, calls=%fused_computation.1 | custom fusion | bytes 8389120 | tf_op jit(solution)/shard_map/jit(_take)/gather | solution.py:214
  200.2 7.1 %select_select_fusion = bf16[128,4,4096]{2,1,0:T(4,128)(2,1)} fusion(bf16[128,4,4096]{2,1,0:T(4,128)(2,1)} %gather_fusion.1, pred[128]{0:T(512)(128)(4,1)S(1)} %compare_and_fusion, pred[128]{0:T(512)(128)(4,1)S(1)} %fusion.22), kind=kLoop, calls=%fused_computation.72 | loop fusion | flops 4194304 | bytes 8388864 | tf_op jit(solution)/shard_map/jit(_where)/select_n | solution.py:214
  207.2 9.8 %all-to-all-start.1 = ((bf16[128,4,4096]{2,1,0:T(4,128)(2,1)}), bf16[128,4,4096]{2,1,0:T(4,128)(2,1)}, u32[]{:S(2)}, u32[]{:S(2)}) async-start(bf16[128,4,4096]{2,1,0:T(4,128)(2,1)} %select_select_fusion), calls=%async_computation.1 | async-start | bytes 8388608 | tf_op jit(solution)/shard_map/all_to_all | solution.py:216
  218.4 92.8 %all-to-all-done.1 = bf16[128,4,4096]{2,1,0:T(4,128)(2,1)} async-done(((bf16[128,4,4096]{2,1,0:T(4,128)(2,1)}), bf16[128,4,4096]{2,1,0:T(4,128)(2,1)}, u32[]{:S(2)}, u32[]{:S(2)}) %all-to-all-start.1) | async-done | bytes 4194336 | tf_op jit(solution)/shard_map/all_to_all | solution.py:216
  311.2 7.9 %copy.86 = bf16[128,4,4096]{0,2,1:T(8,128)(2,1)} copy(bf16[128,4,4096]{2,1,0:T(4,128)(2,1)} %all-to-all-done.1) | data formatting | bytes 8388608 | tf_op jit(solution)/shard_map/all_to_all | solution.py:216
  319.1 3.4 fusion.17
  323.5 2.7 convolution_convert_fusion
  326.2 3.5 copy.88
  329.7 5.5 copy.89
  335.2 6.4 %all-to-all-start.2 = ((bf16[128,3,4096]{2,1,0:T(4,128)(2,1)}), bf16[128,3,4096]{2,1,0:T(4,128)(2,1)}, u32[]{:S(2)}, u32[]{:S(2)}) async-start(bf16[128,3,4096]{2,1,0:T(4,128)(2,1)} %copy.89), calls=%async_computation.2 | async-start | bytes 8388608 | tf_op jit(solution)/shard_map/all_to_all | solution.py:221
  341.7 94.4 %all-to-all-done.2 = bf16[128,3,4096]{2,1,0:T(4,128)(2,1)} async-done(((bf16[128,3,4096]{2,1,0:T(4,128)(2,1)}), bf16[128,3,4096]{2,1,0:T(4,128)(2,1)}, u32[]{:S(2)}, u32[]{:S(2)}) %all-to-all-start.2) | async-done | bytes 3145760 | tf_op jit(solution)/shard_map/all_to_all | solution.py:221
  436.1 4.5 gather_fusion.2
  440.7 2.4 broadcast_select_fusion
  443.1 1.4 broadcast_in_dim.116
  444.4 118.2 %while.24 = (s32[]{:T(128)}, f32[12,64,512]{2,1,0:T(8,128)}, f32[16,64,512]{2,1,0:T(8,128)}, bf16[64,3,4096]{2,1,0:T(4,128)(2,1)}, s32[]{:T(128)}, /*index=5*/s32[]{:T(128)}, s32[]{:T(128)}, s32[]{:T(128)}, s32[]{}) while((s32[]{:T(128)}, f32[12,64,512]{2,1,0:T(8,128)}, f32[16,64,512]{2,1,0:T(8,128)}, bf16[64,3,4096]{2,1,0:T(4,128)(2,1)}, ...), condition=%wide.region_11.12_spmd, body=%wide.region_6.11_spmd.sunk | while | flops 156190720 | bytes 13369515 | solution.py:146
  446.4 1.6 constant_dynamic-slice_fusion.11
  453.8 1.6 constant_dynamic-slice_fusion.11
  461.1 1.6 constant_dynamic-slice_fusion.11
  468.5 1.6 constant_dynamic-slice_fusion.11
  475.9 1.6 constant_dynamic-slice_fusion.11
  483.3 1.6 constant_dynamic-slice_fusion.11
  490.7 1.6 constant_dynamic-slice_fusion.11
  498.0 1.6 constant_dynamic-slice_fusion.11
  505.4 1.6 constant_dynamic-slice_fusion.11
  512.8 1.6 constant_dynamic-slice_fusion.11
  520.2 1.6 constant_dynamic-slice_fusion.11
  527.6 1.6 constant_dynamic-slice_fusion.11
  535.0 1.6 constant_dynamic-slice_fusion.11
  542.4 1.6 constant_dynamic-slice_fusion.11
  549.8 1.6 constant_dynamic-slice_fusion.11
  557.2 1.6 constant_dynamic-slice_fusion.11
  562.6 1.4 slice.120
  565.4 2.5 copy.95
  (700 shorter events, 221.4 us)
Async XLA Ops:
  0.6 2.7 copy-start
  5.7 201.5 %all-to-all-start = ((f32[32,4,1]{1,2,0:T(1,128)}), f32[32,4,1]{1,2,0:T(1,128)S(1)}, u32[]{:S(2)}, u32[]{:S(2)}) async-start(f32[32,4,1]{1,2,0:T(1,128)} %copy.85), calls=%async_computation | async-start | bytes 32768 | tf_op jit(solution)/shard_map/all_to_all | solution.py:217
  19.9 0.9 copy-start.6
  19.9 1.1 copy-start.2
  20.0 1.3 copy-start.3
  20.0 1.5 copy-start.4
  20.8 0.8 copy-start.8
  207.2 104.0 %all-to-all-start.1 = ((bf16[128,4,4096]{2,1,0:T(4,128)(2,1)}), bf16[128,4,4096]{2,1,0:T(4,128)(2,1)}, u32[]{:S(2)}, u32[]{:S(2)}) async-start(bf16[128,4,4096]{2,1,0:T(4,128)(2,1)} %select_select_fusion), calls=%async_computation.1 | async-start | bytes 8388608 | tf_op jit(solution)/shard_map/all_to_all | solution.py:216
  319.1 3.4 copy-start.5
  335.2 6.4 %copy-start.7 = (s32[64,1]{0,1:T(1,128)S(1)}, s32[64,1]{0,1:T(1,128)}, u32[]{:S(2)}) copy-start(s32[64,1]{0,1:T(1,128)} %param.18) | copy-start | bytes 772
  335.2 100.9 %all-to-all-start.2 = ((bf16[128,3,4096]{2,1,0:T(4,128)(2,1)}), bf16[128,3,4096]{2,1,0:T(4,128)(2,1)}, u32[]{:S(2)}, u32[]{:S(2)}) async-start(bf16[128,3,4096]{2,1,0:T(4,128)(2,1)} %copy.89), calls=%async_computation.2 | async-start | bytes 8388608 | tf_op jit(solution)/shard_map/all_to_all | solution.py:221
  565.3 3.6 copy-start.1
where the time goes:
time: 576 us; the launch traced here: 569 us
  waiting for transfers between devices  187 us (32%)
  local copies, waits for them, and re-layouts  160 us (28%)
  other arithmetic  109 us (19%)
  matrix products  70.1 us (12%)
  starting transfers between devices  27.6 us (5%)
  loops' own time  13.9 us (2%)
    all_to_all x1, waiting for transfers between devices, per_device(): lax.all_to_all(cell_rows, ('gy', 'gz'), split_axis=0, concat_axis=0, tile...  94.4 us
    all_to_all x1, waiting for transfers between devices, per_device(): lax.all_to_all(outgoing, ('gy', 'gz'), split_axis=0, concat_axis=0, tiled...  92.8 us
    dot_general x48, matrix products, contract(): jnp.einsum('anp,bnp->nab', flattened, plane, preferred_element_type=jnp.f...  50.1 us
    convert_element_type x32, other arithmetic, outer(): product_table.reshape((EDGE * EDGE,) + product_table.shape[2:])  29 us
    dynamic_slice x16, local copies, waits for them, and re-layouts, interpolate_advance(): lax.dynamic_slice_in_dim(grid_rows, first_block, batch_blocks, 0)  25.8 us
    reshape x16, local copies, waits for them, and re-layouts, interpolate(): flattened = grid_rows.reshape(batch_shape[0], 3 * EDGE, EDGE * EDGE)  16.8 us
    slice x16, local copies, waits for them, and re-layouts, deposit(): affine = particle_data[4:13].reshape((3, 3) + batch_shape)  14.9 us
    another operation x32, other arithmetic  14.9 us
  transfers between devices with their start and end apart: 3, of which 2 were waited for; matrix products, arithmetic and copies ran while one was open for 31% of the time, Pallas kernels for 0%

commit v1 on v0

v1 whole, which is shorter than its diff:
```python
import functools

import jax
import jax.numpy as jnp
from jax import lax
from jax.experimental import pallas as pl
from jax.experimental.pallas import tpu as pltpu
from jax.sharding import PartitionSpec as P

EDGE = 16
QUANT = 1024
PLANE = EDGE * EDGE
STEP_BLOCKS = 8


def stencil(cell_ref, fraction_ref, axis, columns):
    cell = cell_ref[axis : axis + 1, columns].astype(jnp.float32)
    fraction = fraction_ref[axis : axis + 1, columns].astype(jnp.float32)
    position = cell + 0.5 + (fraction + 0.5) / QUANT
    node = lax.broadcasted_iota(jnp.int32, (EDGE, position.shape[1]), 0).astype(jnp.float32)
    offset = node - position
    magnitude = jnp.abs(offset)
    inner = 0.75 - magnitude * magnitude
    reach = jnp.maximum(1.5 - magnitude, 0.0)
    weight = jnp.where(magnitude < 0.5, inner, 0.5 * reach * reach)
    return weight, weight * offset


def fill_planes(cell_ref, fraction_ref, columns, rows_ref, plane_ref):
    width = rows_ref.shape[1]
    weight_y, slope_y = stencil(cell_ref, fraction_ref, 1, columns)
    weight_z, slope_z = stencil(cell_ref, fraction_ref, 2, columns)
    rows_ref[0:EDGE, :] = weight_y
    rows_ref[EDGE : 2 * EDGE, :] = slope_y
    for y in range(EDGE):
        rows = slice(y * EDGE, (y + 1) * EDGE)
        along = rows_ref[y : y + 1, :]
        tilt = rows_ref[EDGE + y : EDGE + y + 1, :]
        plane_ref[rows, 0:width] = (along * weight_z).astype(jnp.bfloat16)
        plane_ref[rows, width : 2 * width] = (tilt * weight_z).astype(jnp.bfloat16)
        plane_ref[rows, 2 * width : 3 * width] = (along * slope_z).astype(jnp.bfloat16)


def deposit_kernel(
    owner_ref,
    slot_ref,
    count_ref,
    mass_ref,
    velocity_ref,
    affine_ref,
    cell_ref,
    fraction_ref,
    deposits_ref,
    place_ref,
    tiles_ref,
    used_ref,
    rows_ref,
    plane_ref,
    lead_ref,
    *,
    capacity,
    width,
):
    step = pl.program_id(0)
    groups = used_ref.shape[0]
    blocks = owner_ref.shape[0]

    @pl.when(step == 0)
    def _():
        deposits_ref[...] = jnp.zeros_like(deposits_ref)
        lead_ref[...] = jnp.zeros_like(lead_ref)

        @pl.loop(0, groups)
        def _(group):
            used_ref[group] = 0

        @pl.loop(0, groups * capacity)
        def _(slot):
            tiles_ref[slot] = -1

        @pl.loop(0, blocks)
        def _(block):
            owner = owner_ref[block]
            rank = used_ref[owner]
            used_ref[owner] = rank + 1
            place = owner * capacity + rank
            place_ref[block] = place
            tiles_ref[place] = slot_ref[block]

    def one_block(local, half):
        block = step * STEP_BLOCKS + local
        columns = pl.ds(pl.multiple_of(local * width, width), width)
        rows_half, plane_half, lead_half = rows_ref.at[half], plane_ref.at[half], lead_ref.at[half]
        fill_planes(cell_ref, fraction_ref, columns, rows_half, plane_half)
        weight, slope = stencil(cell_ref, fraction_ref, 0, columns)
        lane = lax.broadcasted_iota(jnp.int32, (1, width), 1)
        mass = jnp.where(lane < count_ref[block], mass_ref[0:1, columns], 0.0)
        lead_half[0:EDGE, 0:width] = (mass * weight).astype(jnp.bfloat16)
        for d in range(3):
            rows = slice((d + 1) * EDGE, (d + 2) * EDGE)
            velocity = velocity_ref[d : d + 1, columns]
            first = affine_ref[3 * d : 3 * d + 1, columns]
            second = mass * affine_ref[3 * d + 1 : 3 * d + 2, columns]
            third = mass * affine_ref[3 * d + 2 : 3 * d + 3, columns]
            lead_half[rows, 0:width] = (mass * (velocity * weight + first * slope)).astype(jnp.bfloat16)
            lead_half[rows, width : 2 * width] = (second * weight).astype(jnp.bfloat16)
            lead_half[rows, 2 * width : 3 * width] = (third * weight).astype(jnp.bfloat16)
        total = lax.dot_general(
            lead_half[...],
            plane_half[...],
            (((1,), (1,)), ((), ())),
            preferred_element_type=jnp.float32,
        )
        deposits_ref[place_ref[block]] = total.astype(jnp.bfloat16)

    @pl.loop(0, STEP_BLOCKS // 2)
    def _(pair):
        one_block(2 * pair, 0)
        one_block(2 * pair + 1, 1)


def deposit_all(mass, velocity, affine, cell, fraction, owner, slot, count, groups, capacity):
    blocks = owner.shape[0]
    width = mass.shape[0] // blocks
    columns = STEP_BLOCKS * width
    slots = groups * capacity

    def lanes(rows):
        return pl.BlockSpec((rows, columns), lambda i, *_: (0, i))

    return pl.pallas_call(
        functools.partial(deposit_kernel, capacity=capacity, width=width),
        grid_spec=pltpu.PrefetchScalarGridSpec(
            num_scalar_prefetch=3,
            grid=(blocks // STEP_BLOCKS,),
            in_specs=[lanes(1), lanes(3), lanes(9), lanes(3), lanes(3)],
            out_specs=[
                pl.BlockSpec((slots, 4 * EDGE, PLANE), lambda i, *_: (0, 0, 0)),
                pl.BlockSpec(memory_space=pltpu.SMEM),
                pl.BlockSpec(memory_space=pltpu.SMEM),
            ],
            scratch_shapes=[
                pltpu.SMEM((groups,), jnp.int32),
                pltpu.VMEM((2, 2 * EDGE, width), jnp.float32),
                pltpu.VMEM((2, PLANE, 3 * width), jnp.bfloat16),
                pltpu.VMEM((2, 4 * EDGE, 3 * width), jnp.bfloat16),
            ],
        ),
        out_shape=[
            jax.ShapeDtypeStruct((slots, 4 * EDGE, PLANE), jnp.bfloat16),
            jax.ShapeDtypeStruct((blocks,), jnp.int32),
            jax.ShapeDtypeStruct((slots,), jnp.int32),
        ],
        compiler_params=pltpu.CompilerParams(
            dimension_semantics=("arbitrary",), vmem_limit_bytes=40 << 20
        ),
        cost_estimate=pl.CostEstimate(
            flops=2 * blocks * 64 * PLANE * 3 * width, bytes_accessed=7 << 20, transcendentals=0
        ),
        name="deposit",
    )(owner, slot, count, mass.reshape(1, -1), velocity, affine, cell, fraction)


def update_kernel(tiles_ref, arrived_ref, drag_ref, velocity_ref, returned_ref, sums_ref, rounded_ref):
    slots = arrived_ref.shape[0]
    tiles = drag_ref.shape[0]
    sums_ref[...] = jnp.zeros_like(sums_ref)

    @pl.loop(0, slots)
    def _(slot):
        tile = tiles_ref[slot]

        @pl.when(tile >= 0)
        def _():
            sums_ref[tile] = sums_ref[tile] + arrived_ref[slot].astype(jnp.float32)

    @pl.loop(0, tiles)
    def _(tile):
        mass = sums_ref[tile, 0:EDGE, :] + drag_ref[tile]
        for d in range(3):
            rows = slice(d * EDGE, (d + 1) * EDGE)
            value = sums_ref[tile, (d + 1) * EDGE : (d + 2) * EDGE, :] / mass
            velocity_ref[tile, rows, :] = value
            rounded_ref[tile, rows, :] = value.astype(jnp.bfloat16)

    @pl.loop(0, slots)
    def _(slot):
        returned_ref[slot] = rounded_ref[jnp.maximum(tiles_ref[slot], 0)]


def update_grid(arrived, arrived_tiles, drag):
    slots = arrived.shape[0]
    tiles = drag.shape[0]
    whole = pl.BlockSpec(memory_space=pltpu.VMEM)
    return pl.pallas_call(
        update_kernel,
        in_specs=[pl.BlockSpec(memory_space=pltpu.SMEM), whole, whole],
        out_specs=[whole, whole],
        out_shape=[
            jax.ShapeDtypeStruct((tiles, 3 * EDGE, PLANE), jnp.float32),
            jax.ShapeDtypeStruct((slots, 3 * EDGE, PLANE), jnp.bfloat16),
        ],
        scratch_shapes=[
            pltpu.VMEM((tiles, 4 * EDGE, PLANE), jnp.float32),
            pltpu.VMEM((tiles, 3 * EDGE, PLANE), jnp.bfloat16),
        ],
        compiler_params=pltpu.CompilerParams(vmem_limit_bytes=40 << 20),
        cost_estimate=pl.CostEstimate(flops=1 << 24, bytes_accessed=8 << 20, transcendentals=0),
        name="update",
    )(arrived_tiles, arrived, drag)


def sample_kernel(
    place_ref,
    count_ref,
    cell_ref,
    fraction_ref,
    returned_ref,
    velocity_ref,
    affine_ref,
    rows_ref,
    plane_ref,
    *,
    width,
):
    step = pl.program_id(0)

    def one_block(local, half):
        block = step * STEP_BLOCKS + local
        columns = pl.ds(pl.multiple_of(local * width, width), width)
        rows_half, plane_half = rows_ref.at[half], plane_ref.at[half]
        fill_planes(cell_ref, fraction_ref, columns, rows_half, plane_half)
        weight, slope = stencil(cell_ref, fraction_ref, 0, columns)
        moments = jnp.dot(
            returned_ref[place_ref[block]], plane_half[...], preferred_element_type=jnp.float32
        )
        lane = lax.broadcasted_iota(jnp.int32, (1, width), 1)
        present = lane < count_ref[block]

        def gather(d, part, factor):
            moment = moments[d * EDGE : (d + 1) * EDGE, part * width : (part + 1) * width]
            total = jnp.sum(factor * moment, axis=0, keepdims=True)
            return jnp.where(present, total, 0.0)

        for d in range(3):
            velocity_ref[d : d + 1, columns] = gather(d, 0, weight)
            affine_ref[3 * d : 3 * d + 1, columns] = 4.0 * gather(d, 0, slope)
            affine_ref[3 * d + 1 : 3 * d + 2, columns] = 4.0 * gather(d, 1, weight)
            affine_ref[3 * d + 2 : 3 * d + 3, columns] = 4.0 * gather(d, 2, weight)

    @pl.loop(0, STEP_BLOCKS // 2)
    def _(pair):
        one_block(2 * pair, 0)
        one_block(2 * pair + 1, 1)


def sample_all(place, count, cell, fraction, returned):
    blocks = count.shape[0]
    width = cell.shape[1] // blocks
    columns = STEP_BLOCKS * width

    def lanes(rows):
        return pl.BlockSpec((rows, columns), lambda i, *_: (0, i))

    return pl.pallas_call(
        functools.partial(sample_kernel, width=width),
        grid_spec=pltpu.PrefetchScalarGridSpec(
            num_scalar_prefetch=2,
            grid=(blocks // STEP_BLOCKS,),
            in_specs=[lanes(3), lanes(3), pl.BlockSpec(returned.shape, lambda i, *_: (0, 0, 0))],
            out_specs=[lanes(3), lanes(9)],
            scratch_shapes=[
                pltpu.VMEM((2, 2 * EDGE, width), jnp.float32),
                pltpu.VMEM((2, PLANE, 3 * width), jnp.bfloat16),
            ],
        ),
        out_shape=[
            jax.ShapeDtypeStruct((3, cell.shape[1]), jnp.float32),
            jax.ShapeDtypeStruct((9, cell.shape[1]), jnp.float32),
        ],
        compiler_params=pltpu.CompilerParams(
            dimension_semantics=("arbitrary",), vmem_limit_bytes=40 << 20
        ),
        cost_estimate=pl.CostEstimate(
            flops=2 * blocks * 48 * PLANE * 3 * width, bytes_accessed=7 << 20, transcendentals=0
        ),
        name="sample",
    )(place, count, cell, fraction, returned)


def per_device(
    particle_mass,
    particle_velocity,
    particle_affine,
    particle_cell,
    particle_fraction,
    block_owner,
    block_slot,
    block_count,
    cell_drag,
):
    axes = ("gy", "gz")
    groups = lax.axis_size(axes)
    blocks = block_count.shape[0]
    capacity = max(1, 2 * blocks // groups)
    tiles = cell_drag.shape[0]
    deposits, place, tile_ids = deposit_all(
        particle_mass,
        particle_velocity,
        particle_affine,
        particle_cell,
        particle_fraction,
        block_owner.reshape(-1),
        block_slot,
        block_count,
        groups,
        capacity,
    )
    arrived_tiles = lax.all_to_all(tile_ids, axes, split_axis=0, concat_axis=0, tiled=True)
    arrived = lax.all_to_all(deposits, axes, split_axis=0, concat_axis=0, tiled=True)
    drag = cell_drag.reshape(tiles, EDGE, PLANE)
    velocity, answers = update_grid(arrived, arrived_tiles, drag)
    returned = lax.all_to_all(answers, axes, split_axis=0, concat_axis=0, tiled=True)
    new_velocity, new_affine = sample_all(
        place, block_count, particle_cell, particle_fraction, returned
    )
    return (velocity.reshape(tiles, 3, -1), new_velocity, new_affine)


def solution(mesh):
    split = ("gx", "gy", "gz")
    return jax.shard_map(
        per_device,
        mesh=mesh,
        in_specs=(
            P(split),
            P(None, split),
            P(None, split),
            P(None, split),
            P(None, split),
            P(split, None),
            P(split),
            P(split),
            P(split, None),
        ),
        out_specs=(P(split, None, None), P(None, split), P(None, split)),
        check_vma=False,
    )
```

time: 576 us -> 261 us (0.45)
  local copies, waits for them, and re-layouts: 160 us -> 19.9 us
  other arithmetic: 109 us -> 0.69 us
  matrix products: 70.1 us -> 0 us
  Pallas kernels: 0 us -> 47.1 us
  waiting for transfers between devices: 187 us -> 158 us
  blocking collectives: 0 us -> 19.7 us
  starting transfers between devices: 27.6 us -> 12.9 us
  loops' own time: 13.9 us -> 0 us
    dot_general x98 -> x0, matrix products: 70.1 us -> none  [the longest x48 50.1 us: contract(): jnp.einsum('anp,bnp->nab', flattened, plane, preferred_element_type=jnp.f...]
    pallas_call x0 -> x3, Pallas kernels: none -> 47.1 us  [the longest x1 23.5 us: deposit_all(): pl.pallas_call(functools.partial(deposit_kernel, capacity=capacity, width...]
    slice x97 -> x0, local copies, waits for them, and re-layouts: 43.9 us -> none  [the longest x16 14.9 us: deposit(): affine = particle_data[4:13].reshape((3, 3) + batch_shape)]
    dynamic_slice x32 -> x0, local copies, waits for them, and re-layouts: 35.1 us -> none  [the longest x16 25.8 us: interpolate_advance(): lax.dynamic_slice_in_dim(grid_rows, first_block, batch_blocks, 0)]
    convert_element_type x34 -> x0, other arithmetic: 29.8 us -> none  [the longest x32 29 us: outer(): product_table.reshape((EDGE * EDGE,) + product_table.shape[2:])]
    all_to_all x3 -> x2, waiting for transfers between devices: 187 us -> 158 us  [the longest x1 91.9 us: per_device(): lax.all_to_all(deposits, axes, split_axis=0, concat_axis=0, tiled=True)]
    reshape x69 -> x1, local copies, waits for them, and re-layouts: 28.2 us -> 2.36 us  [per_device(): return (velocity.reshape(tiles, 3, -1), new_velocity, new_affine)]
    dynamic_update_slice x32 -> x0, other arithmetic: 23.8 us -> none  [the longest x16 12.8 us: deposit_all(): lax.scan(deposit_advance, jnp.zeros((), jnp.float32), jnp.arange(block_to...]
  transfers between devices with their start and end apart: 3 -> 2, of which waited for: 2 -> 2; matrix products, arithmetic and copies ran while one was open for 31% -> 2% of each run, Pallas kernels for 0% -> 0%
where the time goes in v1:
time: 261 us; the launch traced here: 259 us
  waiting for transfers between devices  158 us (61%)
  Pallas kernels  47.1 us (18%)
  local copies, waits for them, and re-layouts  19.9 us (8%)
  blocking collectives  19.7 us (8%)
  starting transfers between devices  12.9 us (5%)
    all_to_all x1, waiting for transfers between devices, per_device(): lax.all_to_all(deposits, axes, split_axis=0, concat_axis=0, tiled=True)  91.9 us
    all_to_all x1, waiting for transfers between devices, per_device(): lax.all_to_all(answers, axes, split_axis=0, concat_axis=0, tiled=True)  66.3 us
    pallas_call x1, Pallas kernels, deposit_all(): pl.pallas_call(functools.partial(deposit_kernel, capacity=capacity, width...  23.5 us
    all_to_all x1, blocking collectives, per_device(): lax.all_to_all(tile_ids, axes, split_axis=0, concat_axis=0, tiled=True)  19.7 us
    pallas_call x1, Pallas kernels, sample_all(): pl.pallas_call(functools.partial(sample_kernel, width=width), grid_spec=p...  17.8 us
    unnamed x32, local copies, waits for them, and re-layouts  16.8 us
    all_to_all x1, starting transfers between devices, per_device(): lax.all_to_all(answers, axes, split_axis=0, concat_axis=0, tiled=True)  6.94 us
    all_to_all x1, starting transfers between devices, per_device(): lax.all_to_all(deposits, axes, split_axis=0, concat_axis=0, tiled=True)  6.01 us
  transfers between devices with their start and end apart: 2, of which 2 were waited for; matrix products, arithmetic and copies ran while one was open for 2% of the time, Pallas kernels for 0%

profile of v1, /device:TPU:34, one launch (start us, length us, event | category | flops | bytes accessed | tf_op | source)
XLA Modules:
  0.0 259.2 jit_solution(18199152068382015634)
XLA Ops:
  0.6 0.0 copy-start.3
  0.6 1.6 copy-done.3
  2.2 0.0 copy-start.4
  2.2 1.0 copy-done.4
  3.3 0.0 copy-start.5
  3.3 1.0 copy-done.5
  4.3 0.0 copy-start.7
  4.3 1.0 copy-done.7
  5.3 0.0 copy-start.9
  5.4 0.9 copy-done.9
  6.3 0.0 copy-start.10
  6.3 0.7 copy-done.10
  6.9 0.0 copy-start.11
  6.9 0.7 copy-done.11
  7.6 0.0 copy-start.12
  7.6 0.7 copy-done.12
  8.2 23.5 %deposit.1 = (bf16[128,64,256]{2,1,0:T(8,128)(2,1)S(1)}, s32[64]{0:T(128)S(1)}, s32[128]{0:T(128)S(1)}) custom-call(s32[64]{0:T(128)S(1)} %bitcast.8, s32[64]{0:T(128)S(1)} %copy-done.11, s32[64]{0:T(128)S(1)} %copy-done.12, f32[1,32768]{1,0:T(1,128)S(1)} %bitcast.7, f32[3,32768]{1,0:T(4,128)S(1)} %copy-done.4, f32[9,32768]{1,0:T(8,128)S(1)} %copy-done.3, ...), custom_call_target="tpu_custom_call" | custom-call | flops 3221225472 | bytes 7340032 | tf_op jit(solution)/shard_map/deposit/pallas_call | solution.py:131
  31.8 0.0 copy-start
  31.8 2.0 copy-done
  33.8 0.1 all_to_all.13
  33.9 19.7 %all_to_all.21 = s32[32,4,1]{1,2,0:T(1,128)S(1)} all-to-all(s32[32,4,1]{1,2,0:T(1,128)S(1)} %bitcast.10), channel_id=1, replica_groups=mesh['gx'=8,'gy'=8,'gz'=4] {'gy','gz'}, dimensions={0} | all-to-all | bytes 1024 | tf_op jit(solution)/shard_map/all_to_all | solution.py:319
  53.6 0.0 copy-start.14
  53.6 6.0 %all-to-all-start.1 = ((bf16[128,64,256]{2,1,0:T(8,128)(2,1)}), bf16[128,64,256]{2,1,0:T(8,128)(2,1)}, u32[]{:S(2)}, u32[]{:S(2)}) async-start(bf16[128,64,256]{2,1,0:T(8,128)(2,1)} %copy-done), calls=%async_computation.1 | async-start | bytes 8388608 | tf_op jit(solution)/shard_map/all_to_all | solution.py:320
  59.6 0.0 copy-done.14
  59.6 0.1 copy.16
  59.7 0.5 broadcast.3
  60.2 0.7 reduce.3
  60.9 0.1 all_to_all.15.tiles_ref
  61.0 91.9 %all-to-all-done.1.arrived_ref = bf16[128,64,256]{2,1,0:T(8,128)(2,1)} async-done(((bf16[128,64,256]{2,1,0:T(8,128)(2,1)}), bf16[128,64,256]{2,1,0:T(8,128)(2,1)}, u32[]{:S(2)}, u32[]{:S(2)}) %all-to-all-start.1) | async-done | bytes 4194336 | tf_op jit(solution)/shard_map/all_to_all | solution.py:320
  152.9 5.7 %update.1 = (f32[16,48,256]{2,1,0:T(8,128)S(1)}, bf16[128,48,256]{2,1,0:T(8,128)(2,1)S(1)}) custom-call(s32[128]{0:T(128)S(1)} %all_to_all.15.tiles_ref, bf16[128,64,256]{2,1,0:T(8,128)(2,1)} %all-to-all-done.1.arrived_ref, f32[16,16,256]{2,1,0:T(8,128)S(1)} %bitcast.6), custom_call_target="tpu_custom_call" | custom-call | flops 16777216 | bytes 8388608 | tf_op jit(solution)/shard_map/update/pallas_call | solution.py:195
  158.7 0.0 copy-start.1
  158.7 1.6 copy-done.1
  160.3 0.0 copy-start.2
  160.3 0.9 copy-done.2
  161.2 6.9 %all-to-all-start.2 = ((bf16[128,48,256]{2,1,0:T(8,128)(2,1)}), bf16[128,48,256]{2,1,0:T(8,128)(2,1)S(1)}, u32[]{:S(2)}, u32[]{:S(2)}) async-start(bf16[128,48,256]{2,1,0:T(8,128)(2,1)} %copy-done.1), calls=%async_computation.2 | async-start | bytes 6291456 | tf_op jit(solution)/shard_map/all_to_all | solution.py:323
  168.1 0.0 copy-start.13
  168.1 2.4 reshape.23
  170.5 2.6 copy.15
  173.1 66.3 %all-to-all-done.2.returned_ref = bf16[128,48,256]{2,1,0:T(8,128)(2,1)S(1)} async-done(((bf16[128,48,256]{2,1,0:T(8,128)(2,1)}), bf16[128,48,256]{2,1,0:T(8,128)(2,1)S(1)}, u32[]{:S(2)}, u32[]{:S(2)}) %all-to-all-start.2) | async-done | bytes 3145760 | tf_op jit(solution)/shard_map/all_to_all | solution.py:323
  239.3 0.0 copy-done.13
  239.3 0.0 copy-start.6
  239.3 1.0 copy-done.6
  240.4 0.0 copy-start.8
  240.4 1.0 copy-done.8
  241.4 17.8 %sample.1 = (f32[3,32768]{1,0:T(4,128)}, f32[9,32768]{1,0:T(8,128)}) custom-call(s32[64]{0:T(128)S(1)} %get-tuple-element.13.place_ref, s32[64]{0:T(128)S(1)} %copy-done.13, s32[3,32768]{1,0:T(4,128)S(1)} %copy-done.6, s32[3,32768]{1,0:T(4,128)S(1)} %copy-done.8, bf16[128,48,256]{2,1,0:T(8,128)(2,1)S(1)} %all-to-all-done.2.returned_ref), custom_call_target="tpu_custom_call" | custom-call | flops 2415919104 | bytes 7340032 | tf_op jit(solution)/shard_map/sample/pallas_call | solution.py:265
Async XLA Ops:
  0.6 1.6 copy-start.3
  2.2 1.0 copy-start.4
  3.3 1.0 copy-start.5
  4.3 1.0 copy-start.7
  5.3 0.9 copy-start.9
  6.3 0.7 copy-start.10
  6.9 0.7 copy-start.11
  7.6 0.7 copy-start.12
  31.8 2.0 copy-start
  53.6 6.0 %copy-start.14 = (f32[16,4096]{1,0:T(8,128)S(1)}, f32[16,4096]{1,0:T(8,128)}, u32[]{:S(2)}) copy-start(f32[16,4096]{1,0:T(8,128)} %param.17) | copy-start | bytes 786436
  53.6 99.3 %all-to-all-start.1 = ((bf16[128,64,256]{2,1,0:T(8,128)(2,1)}), bf16[128,64,256]{2,1,0:T(8,128)(2,1)}, u32[]{:S(2)}, u32[]{:S(2)}) async-start(bf16[128,64,256]{2,1,0:T(8,128)(2,1)} %copy-done), calls=%async_computation.1 | async-start | bytes 8388608 | tf_op jit(solution)/shard_map/all_to_all | solution.py:320
  158.7 1.6 copy-start.1
  160.3 0.9 copy-start.2
  161.2 78.1 %all-to-all-start.2 = ((bf16[128,48,256]{2,1,0:T(8,128)(2,1)}), bf16[128,48,256]{2,1,0:T(8,128)(2,1)S(1)}, u32[]{:S(2)}, u32[]{:S(2)}) async-start(bf16[128,48,256]{2,1,0:T(8,128)(2,1)} %copy-done.1), calls=%async_computation.2 | async-start | bytes 6291456 | tf_op jit(solution)/shard_map/all_to_all | solution.py:323
  168.1 71.2 %copy-start.13 = (s32[64]{0:T(128)S(1)}, s32[64]{0:T(128)}, u32[]{:S(2)}) copy-start(s32[64]{0:T(128)} %count_ref.3) | copy-start | bytes 772
  239.3 1.0 copy-start.6
  240.4 1.0 copy-start.8

commit v2 on v1

--- a/solution.py
+++ b/solution.py
@@ -10,6 +10,9 @@
 EDGE = 16
 QUANT = 1024
 PLANE = EDGE * EDGE
+LANES = 128
+CHUNK = 4
+MESH = pl.DeviceIdType.MESH
 STEP_BLOCKS = 8
 
 
@@ -51,8 +54,8 @@
     cell_ref,
     fraction_ref,
     deposits_ref,
+    names_ref,
     place_ref,
-    tiles_ref,
     used_ref,
     rows_ref,
     plane_ref,
@@ -60,6 +63,7 @@
     *,
     capacity,
     width,
+    columns_of,
 ):
     step = pl.program_id(0)
     groups = used_ref.shape[0]
@@ -69,23 +73,22 @@
     def _():
         deposits_ref[...] = jnp.zeros_like(deposits_ref)
         lead_ref[...] = jnp.zeros_like(lead_ref)
+        names_ref[...] = jnp.full_like(names_ref, -1.0)
 
         @pl.loop(0, groups)
         def _(group):
             used_ref[group] = 0
-
-        @pl.loop(0, groups * capacity)
-        def _(slot):
-            tiles_ref[slot] = -1
 
         @pl.loop(0, blocks)
         def _(block):
             owner = owner_ref[block]
             rank = used_ref[owner]
             used_ref[owner] = rank + 1
-            place = owner * capacity + rank
+            row = lax.rem(owner, columns_of) * (groups // columns_of) + lax.div(owner, columns_of)
+            place = row * capacity + rank
             place_ref[block] = place
-            tiles_ref[place] = slot_ref[block]
+            name = lax.convert_element_type(slot_ref[block], jnp.float32)
+            names_ref[pl.ds(place, 1), :] = jnp.full((1, names_ref.shape[1]), name, jnp.float32)
 
     def one_block(local, half):
         block = step * STEP_BLOCKS + local
@@ -119,7 +122,7 @@
         one_block(2 * pair + 1, 1)
 
 
-def deposit_all(mass, velocity, affine, cell, fraction, owner, slot, count, groups, capacity):
+def deposit_all(mass, velocity, affine, cell, fraction, owner, slot, count, groups, capacity, columns_of):
     blocks = owner.shape[0]
     width = mass.shape[0] // blocks
     columns = STEP_BLOCKS * width
@@ -129,14 +132,16 @@
         return pl.BlockSpec((rows, columns), lambda i, *_: (0, i))
 
     return pl.pallas_call(
-        functools.partial(deposit_kernel, capacity=capacity, width=width),
+        functools.partial(
+            deposit_kernel, capacity=capacity, width=width, columns_of=columns_of
+        ),
         grid_spec=pltpu.PrefetchScalarGridSpec(
             num_scalar_prefetch=3,
             grid=(blocks // STEP_BLOCKS,),
             in_specs=[lanes(1), lanes(3), lanes(9), lanes(3), lanes(3)],
             out_specs=[
                 pl.BlockSpec((slots, 4 * EDGE, PLANE), lambda i, *_: (0, 0, 0)),
-                pl.BlockSpec(memory_space=pltpu.SMEM),
+                pl.BlockSpec((slots, LANES), lambda i, *_: (0, 0)),
                 pl.BlockSpec(memory_space=pltpu.SMEM),
             ],
             scratch_shapes=[
@@ -148,8 +153,8 @@
         ),
         out_shape=[
             jax.ShapeDtypeStruct((slots, 4 * EDGE, PLANE), jnp.bfloat16),
+            jax.ShapeDtypeStruct((slots, LANES), jnp.float32),
             jax.ShapeDtypeStruct((blocks,), jnp.int32),
-            jax.ShapeDtypeStruct((slots,), jnp.int32),
         ],
         compiler_params=pltpu.CompilerParams(
             dimension_semantics=("arbitrary",), vmem_limit_bytes=40 << 20
@@ -161,53 +166,407 @@
     )(owner, slot, count, mass.reshape(1, -1), velocity, affine, cell, fraction)
 
 
-def update_kernel(tiles_ref, arrived_ref, drag_ref, velocity_ref, returned_ref, sums_ref, rounded_ref):
-    slots = arrived_ref.shape[0]
+def exchange_kernel(
+    deposits_ref,
+    names_ref,
+    drag_ref,
+    velocity_ref,
+    back_ref,
+    slot_in,
+    name_in,
+    relay,
+    part_out,
+    part_in,
+    own_names,
+    table,
+    own_sum,
+    grid_all,
+    reply,
+    relay_back,
+    name_send,
+    name_recv,
+    out_send,
+    out_recv,
+    part_send,
+    part_recv,
+    grid_send,
+    grid_recv,
+    back_send,
+    back_recv,
+):
+    side, ring, capacity = deposits_ref.shape[:3]
     tiles = drag_ref.shape[0]
-    sums_ref[...] = jnp.zeros_like(sums_ref)
-
-    @pl.loop(0, slots)
-    def _(slot):
-        tile = tiles_ref[slot]
-
-        @pl.when(tile >= 0)
-        def _():
-            sums_ref[tile] = sums_ref[tile] + arrived_ref[slot].astype(jnp.float32)
-
-    @pl.loop(0, tiles)
-    def _(tile):
-        mass = sums_ref[tile, 0:EDGE, :] + drag_ref[tile]
-        for d in range(3):
-            rows = slice(d * EDGE, (d + 1) * EDGE)
-            value = sums_ref[tile, (d + 1) * EDGE : (d + 2) * EDGE, :] / mass
-            velocity_ref[tile, rows, :] = value
-            rounded_ref[tile, rows, :] = value.astype(jnp.bfloat16)
-
-    @pl.loop(0, slots)
-    def _(slot):
-        returned_ref[slot] = rounded_ref[jnp.maximum(tiles_ref[slot], 0)]
-
-
-def update_grid(arrived, arrived_tiles, drag):
-    slots = arrived.shape[0]
+    chunks = tiles // CHUNK
+    half = capacity // 2
+    steps = ring // 2
+    g, q = lax.axis_index("gy"), lax.axis_index("gz")
+    q_up, q_down, q_far = lax.rem(q + 1, side), lax.rem(q + side - 1, side), lax.rem(q + 2, side)
+    up, down, far = {"gz": q_up}, {"gz": q_down}, {"gz": q_far}
+    along = ({"gy": lax.rem(g + 1, ring)}, {"gy": lax.rem(g + ring - 1, ring)})
+
+    def at(delta):
+        return lax.rem(g + delta + ring, ring)
+
+    def copy(source, target, send, recv, device):
+        return pltpu.make_async_remote_copy(
+            src_ref=source,
+            dst_ref=target,
+            send_sem=send,
+            recv_sem=recv,
+            device_id=device,
+            device_id_type=MESH,
+        )
+
+    barrier = pltpu.get_barrier_semaphore()
+    peers = (up, down, far) + along
+    for peer in peers:
+        pl.semaphore_signal(barrier, inc=1, device_id=peer, device_id_type=MESH)
+    pl.semaphore_wait(barrier, len(peers))
+
+    name_copies = [
+        copy(names_ref.at[there], name_in.at[k], name_send.at[k], name_recv.at[k], device)
+        for k, (there, device) in enumerate(((q_up, up), (q_down, down), (q_far, far)))
+    ]
+    for item in name_copies:
+        item.start()
+
+    order = [(4, None, 0), (3, 0, 1), (-3, 1, 1), (2, 0, 2), (-2, 1, 2), (1, 0, 3), (-1, 1, 3), (0, None, 4)]
+    owners = [at(delta) for delta, _, _ in order]
+
+    def outward(i):
+        o = owners[i]
+        return [
+            copy(deposits_ref.at[q_up, o], slot_in.at[0, o], out_send.at[i, 0], out_recv.at[i, 0], up),
+            copy(deposits_ref.at[q_down, o], slot_in.at[1, o], out_send.at[i, 1], out_recv.at[i, 1], down),
+            copy(
+                deposits_ref.at[q_far, o, pl.ds(0, half)],
+                relay.at[0, o],
+                out_send.at[i, 2],
+                out_recv.at[i, 2],
+                up,
+            ),
+            copy(
+                deposits_ref.at[q_far, o, pl.ds(half, half)],
+                relay.at[1, o],
+                out_send.at[i, 3],
+                out_recv.at[i, 3],
+                down,
+            ),
+            copy(
+                relay.at[0, o],
+                slot_in.at[2, o, pl.ds(0, half)],
+                out_send.at[i, 4],
+                out_recv.at[i, 4],
+                up,
+            ),
+            copy(
+                relay.at[1, o],
+                slot_in.at[2, o, pl.ds(half, half)],
+                out_send.at[i, 5],
+                out_recv.at[i, 5],
+                down,
+            ),
+        ]
+
+    out = [outward(i) for i in range(ring)]
+
+    def first_hop(i):
+        if i < ring:
+            for item in out[i][:4]:
+                item.start()
+
+    def second_hop(i):
+        if i < ring:
+            for k in (0, 1):
+                out[i][2 + k].wait_recv()
+                out[i][4 + k].start()
+
+    def part_copy(way, e, c):
+        rows = pl.ds(c * CHUNK, CHUNK)
+        return copy(
+            part_out.at[way, e, rows],
+            part_in.at[way, e, rows],
+            part_send.at[way, e, c],
+            part_recv.at[way, e, c],
+            along[way],
+        )
+
+    def prepare(i):
+        o = owners[i]
+        for role in range(4):
+            source = names_ref.at[q] if role == 3 else name_in.at[role]
+            for r in range(capacity):
+                row = role * capacity + r
+                own_names[row : row + 1, :] = source[pl.ds(o * capacity + r, 1), :]
+        named = own_names[...]
+        for t in range(tiles):
+            table[i, t] = jnp.where(named == float(t), 1.0, 0.0)
+
+    def add_up(i, c, incoming, put):
+        o = owners[i]
+
+        @pl.loop(0, 4)
+        def _(d):
+            rows = pl.ds(pl.multiple_of(d * EDGE, EDGE), EDGE)
+            sums = [None] * CHUNK
+            for role in range(4):
+                for r in range(capacity):
+                    source = deposits_ref.at[q, o, r] if role == 3 else slot_in.at[role, o, r]
+                    value = source[rows, :].astype(jnp.float32)
+                    row = role * capacity + r
+                    for t in range(CHUNK):
+                        factor = table[i, c * CHUNK + t, row : row + 1, :]
+                        term = jnp.concatenate([factor, factor], axis=1) * value
+                        sums[t] = term if sums[t] is None else sums[t] + term
+            for t in range(CHUNK):
+                total = sums[t]
+                for way, e in incoming:
+                    total = total + part_in[way, e, c * CHUNK + t, rows, :].astype(jnp.float32)
+                put(c, t, rows, total)
+
+    def send_parts(i, way, e, first, last, incoming):
+        @pl.loop(first, last)
+        def _(k):
+            c = lax.rem(k + way * (chunks // 2), chunks)
+            for w, before in incoming:
+                part_copy(w, before, c).wait_recv()
+
+            def put(c, t, rows, total):
+                part_out[way, e, c * CHUNK + t, rows, :] = total.astype(jnp.bfloat16)
+
+            add_up(i, c, incoming, put)
+            part_copy(way, e, c).start()
+
+    first_hop(0)
+    first_hop(1)
+    for item in name_copies:
+        item.wait_recv()
+    second_hop(0)
+    first_hop(2)
+    for i, (_, way, e) in enumerate(order):
+        second_hop(i + 1)
+        first_hop(i + 3)
+        prepare(i)
+        for k in (0, 1, 4, 5):
+            out[i][k].wait_recv()
+        if e == 0:
+            send_parts(i, 0, 0, 0, chunks // 2, ())
+            send_parts(i, 1, 0, 0, chunks // 2, ())
+        elif e == 1:
+            send_parts(i, way, e, 0, chunks // 2, ((way, 0),))
+            send_parts(i, way, e, chunks // 2, chunks, ())
+        elif e < steps:
+            send_parts(i, way, e, 0, chunks, ((way, e - 1),))
+
+    def grid_copy(way, e, c):
+        o = at(-e) if way == 0 else at(e)
+        rows = pl.ds(c * CHUNK, CHUNK)
+        return copy(
+            grid_all.at[o, rows],
+            grid_all.at[o, rows],
+            grid_send.at[way, e, c],
+            grid_recv.at[way, e, c],
+            along[way],
+        )
+
+    @pl.loop(0, chunks)
+    def _(c):
+        for way in (0, 1):
+            part_copy(way, steps - 1, c).wait_recv()
+
+        def put(c, t, rows, total):
+            own_sum[t, rows, :] = total
+
+        add_up(ring - 1, c, ((0, steps - 1), (1, steps - 1)), put)
+        for t in range(CHUNK):
+            tile = c * CHUNK + t
+            mass = own_sum[t, 0:EDGE, :] + drag_ref[tile]
+            for d in range(3):
+                rows = slice(d * EDGE, (d + 1) * EDGE)
+                value = own_sum[t, (d + 1) * EDGE : (d + 2) * EDGE, :] / mass
+                velocity_ref[tile, rows, :] = value
+                grid_all[g, tile, rows, :] = value.astype(jnp.bfloat16)
+        for way in (0, 1):
+            grid_copy(way, 0, c).start()
+
+    def inward(i):
+        o = owners[i]
+        return [
+            copy(reply.at[1, o], back_ref.at[q, o], back_send.at[i, 0], back_recv.at[i, 0], up),
+            copy(reply.at[0, o], back_ref.at[q, o], back_send.at[i, 1], back_recv.at[i, 1], down),
+            copy(
+                reply.at[2, o, pl.ds(0, half)],
+                relay_back.at[0, o],
+                back_send.at[i, 2],
+                back_recv.at[i, 2],
+                up,
+            ),
+            copy(
+                reply.at[2, o, pl.ds(half, half)],
+                relay_back.at[1, o],
+                back_send.at[i, 3],
+                back_recv.at[i, 3],
+                down,
+            ),
+            copy(
+                relay_back.at[0, o],
+                back_ref.at[q_down, o, pl.ds(0, half)],
+                back_send.at[i, 4],
+                back_recv.at[i, 4],
+                up,
+            ),
+            copy(
+                relay_back.at[1, o],
+                back_ref.at[q_up, o, pl.ds(half, half)],
+                back_send.at[i, 5],
+                back_recv.at[i, 5],
+                down,
+            ),
+        ]
+
+    replies = [inward(i) for i in range(ring)]
+
+    def pick(i, role, r, target):
+        o = owners[i]
+        row = role * capacity + r
+        total = None
+        for t in range(tiles):
+            factor = jnp.broadcast_to(table[i, t, pl.ds(row, 1), :], (EDGE, LANES)).astype(jnp.bfloat16)
+            factor = jnp.concatenate([factor, factor], axis=1)
+            factor = jnp.concatenate([factor] * 3, axis=0)
+            term = factor * grid_all[o, t]
+            total = term if total is None else total + term
+        target[...] = total
+
+    def answer(i):
+        o = owners[i]
+
+        @pl.loop(0, capacity)
+        def _(r):
+            for role in range(3):
+                pick(i, role, r, reply.at[role, o, r])
+            pick(i, 3, r, back_ref.at[q, o, r])
+
+        for item in replies[i][:4]:
+            item.start()
+
+    def pass_back(i):
+        for k in (0, 1):
+            replies[i][2 + k].wait_recv()
+            replies[i][4 + k].start()
+
+    answer(ring - 1)
+    waiting = [ring - 1]
+    for e in range(steps):
+        last = e == steps - 1
+
+        def take(first, stop):
+            @pl.loop(first, stop)
+            def _(k):
+                for way in (0, 1):
+                    c = lax.rem(k + way * (chunks // 2), chunks)
+                    grid_copy(way, e, c).wait_recv()
+                    if e + 1 < steps - 1:
+                        grid_copy(way, e + 1, c).start()
+
+        def take_final(first, stop):
+            @pl.loop(first, stop)
+            def _(k):
+                for way in (0, 1):
+                    c = lax.rem(k + way * (chunks // 2), chunks)
+                    grid_copy(way, e, c).wait_recv()
+                    grid_copy(way, e + 1, c).start()
+
+        if last:
+            for i in waiting:
+                pass_back(i)
+            take(0, chunks // 2)
+            now = [0]
+        else:
+            if e + 1 == steps - 1:
+                take_final(0, chunks // 2)
+            else:
+                take(0, chunks // 2)
+            for i in waiting:
+                pass_back(i)
+            take(chunks // 2, chunks)
+            now = [ring - 2 - 2 * e, ring - 3 - 2 * e]
+        for i in now:
+            answer(i)
+        waiting = now
+    for i in waiting:
+        pass_back(i)
+
+    for i in range(ring):
+        for k in (0, 1, 4, 5):
+            replies[i][k].wait_recv()
+    for item in name_copies:
+        item.wait_send()
+    for i in range(ring):
+        for k in range(6):
+            out[i][k].wait_send()
+            replies[i][k].wait_send()
+    for way in (0, 1):
+        for e in range(1, steps):
+
+            @pl.loop(0, chunks)
+            def _(c):
+                part_copy(way, e, c).wait_send()
+                grid_copy(way, e - 1, c).wait_send()
+
+        @pl.loop(0, chunks // 2)
+        def _(k):
+            c = k + way * (chunks // 2)
+            part_copy(way, 0, c).wait_send()
+            grid_copy(way, steps - 1, c).wait_send()
+
+
+def exchange(deposits, names, drag):
+    side, ring, capacity = deposits.shape[:3]
     tiles = drag.shape[0]
+    steps = ring // 2
+    chunks = tiles // CHUNK
+    half = capacity // 2
     whole = pl.BlockSpec(memory_space=pltpu.VMEM)
+    dma = pltpu.SemaphoreType.DMA
+    block, answer = (4 * EDGE, PLANE), (3 * EDGE, PLANE)
     return pl.pallas_call(
-        update_kernel,
-        in_specs=[pl.BlockSpec(memory_space=pltpu.SMEM), whole, whole],
-        out_specs=[whole, whole],
+        exchange_kernel,
+        in_specs=[whole] * 3,
+        out_specs=[whole] * 2,
         out_shape=[
-            jax.ShapeDtypeStruct((tiles, 3 * EDGE, PLANE), jnp.float32),
-            jax.ShapeDtypeStruct((slots, 3 * EDGE, PLANE), jnp.bfloat16),
+            jax.ShapeDtypeStruct((tiles,) + answer, jnp.float32),
+            jax.ShapeDtypeStruct((side, ring, capacity) + answer, jnp.bfloat16),
         ],
         scratch_shapes=[
-            pltpu.VMEM((tiles, 4 * EDGE, PLANE), jnp.float32),
-            pltpu.VMEM((tiles, 3 * EDGE, PLANE), jnp.bfloat16),
+            pltpu.VMEM((3, ring, capacity) + block, jnp.bfloat16),
+            pltpu.VMEM((3,) + names.shape[1:], jnp.float32),
+            pltpu.VMEM((2, ring, half) + block, jnp.bfloat16),
+            pltpu.VMEM((2, steps, tiles) + block, jnp.bfloat16),
+            pltpu.VMEM((2, steps, tiles) + block, jnp.bfloat16),
+            pltpu.VMEM((4 * capacity, LANES), jnp.float32),
+            pltpu.VMEM((ring, tiles, 4 * capacity, LANES), jnp.float32),
+            pltpu.VMEM((CHUNK,) + block, jnp.float32),
+            pltpu.VMEM((ring, tiles) + answer, jnp.bfloat16),
+            pltpu.VMEM((3, ring, capacity) + answer, jnp.bfloat16),
+            pltpu.VMEM((2, ring, half) + answer, jnp.bfloat16),
+            dma((3,)),
+            dma((3,)),
+            dma((ring, 6)),
+            dma((ring, 6)),
+            dma((2, steps, chunks)),
+            dma((2, steps, chunks)),
+            dma((2, steps, chunks)),
+            dma((2, steps, chunks)),
+            dma((ring, 6)),
+            dma((ring, 6)),
         ],
-        compiler_params=pltpu.CompilerParams(vmem_limit_bytes=40 << 20),
-        cost_estimate=pl.CostEstimate(flops=1 << 24, bytes_accessed=8 << 20, transcendentals=0),
-        name="update",
-    )(arrived_tiles, arrived, drag)
+        compiler_params=pltpu.CompilerParams(
+            collective_id=0, has_side_effects=True, vmem_limit_bytes=56 << 20
+        ),
+        cost_estimate=pl.CostEstimate(flops=1 << 26, bytes_accessed=8 << 20, transcendentals=0),
+        name="exchange",
+    )(deposits, names, drag)
 
 
 def sample_kernel(
@@ -299,12 +658,12 @@
     block_count,
     cell_drag,
 ):
-    axes = ("gy", "gz")
-    groups = lax.axis_size(axes)
+    ring, side = lax.axis_size("gy"), lax.axis_size("gz")
+    groups = ring * side
     blocks = block_count.shape[0]
     capacity = max(1, 2 * blocks // groups)
     tiles = cell_drag.shape[0]
-    deposits, place, tile_ids = deposit_all(
+    deposits, names, place = deposit_all(
         particle_mass,
         particle_velocity,
         particle_affine,
@@ -315,14 +674,19 @@
         block_count,
         groups,
         capacity,
+        side,
     )
-    arrived_tiles = lax.all_to_all(tile_ids, axes, split_axis=0, concat_axis=0, tiled=True)
-    arrived = lax.all_to_all(deposits, axes, split_axis=0, concat_axis=0, tiled=True)
-    drag = cell_drag.reshape(tiles, EDGE, PLANE)
-    velocity, answers = update_grid(arrived, arrived_tiles, drag)
-    returned = lax.all_to_all(answers, axes, split_axis=0, concat_axis=0, tiled=True)
+    velocity, back = exchange(
+        deposits.reshape(side, ring, capacity, 4 * EDGE, PLANE),
+        names.reshape(side, ring * capacity, LANES),
+        cell_drag.reshape(tiles, EDGE, PLANE),
+    )
     new_velocity, new_affine = sample_all(
-        place, block_count, particle_cell, particle_fraction, returned
+        place,
+        block_count,
+        particle_cell,
+        particle_fraction,
+        back.reshape(groups * capacity, 3 * EDGE, PLANE),
     )
     return (velocity.reshape(tiles, 3, -1), new_velocity, new_affine)
 

time: 261 us -> 179 us (0.69)
  the two profiles are of different devices: /device:TPU:34 before, /device:TPU:4 now
where the time goes in v2:
time: 179 us
  Pallas kernels  162 us (91%)
  local copies, waits for them, and re-layouts  15.6 us (9%)
    pallas_call x1, Pallas kernels, exchange(): pl.pallas_call(exchange_kernel, in_specs=[whole] * 3, out_specs=[whole] *...  122 us
    pallas_call x1, Pallas kernels, deposit_all(): pl.pallas_call(functools.partial(deposit_kernel, capacity=capacity, width...  22.9 us
    pallas_call x1, Pallas kernels, sample_all(): pl.pallas_call(functools.partial(sample_kernel, width=width), grid_spec=p...  17.8 us
    unnamed x32, local copies, waits for them, and re-layouts  15.1 us

profile of v2, /device:TPU:4, one launch (start us, length us, event | category | flops | bytes accessed | tf_op | source)
XLA Modules:
  0.0 178.5 jit_solution(17182567799750498440)
XLA Ops:
  0.6 1.7 copy.14
  2.4 0.0 copy-start.3
  2.4 1.6 copy-done.3
  4.0 0.0 copy-start.4
  4.0 1.0 copy-done.4
  5.0 0.0 copy-start.5
  5.0 1.0 copy-done.5
  6.0 0.0 copy-start.7
  6.0 1.0 copy-done.7
  7.1 0.0 copy-start.9
  7.1 0.9 copy-done.9
  8.0 0.0 copy-start.10
  8.0 0.7 copy-done.10
  8.6 0.0 copy-start.11
  8.6 0.7 copy-done.11
  9.3 0.0 copy-start.12
  9.3 0.7 copy-done.12
  10.0 22.9 %deposit.1 = (bf16[128,64,256]{2,1,0:T(8,128)(2,1)S(1)}, f32[128,128]{1,0:T(8,128)S(1)}, s32[64]{0:T(128)S(1)}) custom-call(s32[64]{0:T(128)S(1)} %bitcast.11, s32[64]{0:T(128)S(1)} %copy-done.11, s32[64]{0:T(128)S(1)} %copy-done.12, f32[1,32768]{1,0:T(1,128)S(1)} %bitcast.10, f32[3,32768]{1,0:T(4,128)S(1)} %copy-done.4, f32[9,32768]{1,0:T(8,128)S(1)} %copy-done.3, ...), custom_call_target="tpu_custom_call" | custom-call | flops 3221225472 | bytes 7340032 | tf_op jit(solution)/shard_map/deposit/pallas_call | solution.py:134
  32.9 0.0 copy-start
  32.9 2.0 %copy-done = bf16[128,64,256]{2,1,0:T(8,128)(2,1)} copy-done((bf16[128,64,256]{2,1,0:T(8,128)(2,1)}, bf16[128,64,256]{2,1,0:T(8,128)(2,1)S(1)}, u32[]{:S(2)}) %copy-start) | copy-done | bytes 4194328
  34.9 0.0 copy-start.1
  34.9 0.6 copy-done.1
  35.5 0.0 copy-start.6
  35.5 0.0 copy-start.8
  35.5 0.0 copy-start.13
  35.5 121.6 %exchange.1 = (f32[16,48,256]{2,1,0:T(8,128)}, bf16[4,8,4,48,256]{4,3,2,1,0:T(8,128)(2,1)}) custom-call(bf16[4,8,4,64,256]{4,3,2,1,0:T(8,128)(2,1)} %bitcast.7, f32[4,32,128]{2,1,0:T(8,128)} %bitcast.8, f32[16,16,256]{2,1,0:T(8,128)} %bitcast.12), custom_call_target="tpu_custom_call" | custom-call | flops 67108864 | bytes 8388608 | tf_op jit(solution)/shard_map/exchange/pallas_call | solution.py:533
  157.1 0.0 copy-done.6
  157.1 0.0 copy-done.8
  157.1 0.0 copy-done.13
  157.1 0.0 copy-start.2
  157.1 1.9 %copy-done.2 = bf16[4,8,4,48,256]{4,3,2,1,0:T(8,128)(2,1)S(1)} copy-done((bf16[4,8,4,48,256]{4,3,2,1,0:T(8,128)(2,1)S(1)}, bf16[4,8,4,48,256]{4,3,2,1,0:T(8,128)(2,1)}, u32[]{:S(2)}) %copy-start.2) | copy-done | bytes 3145752
  159.0 0.0 copy-start.14
  159.0 17.8 %sample.1 = (f32[3,32768]{1,0:T(4,128)}, f32[9,32768]{1,0:T(8,128)}) custom-call(s32[64]{0:T(128)S(1)} %get-tuple-element.13.place_ref, s32[64]{0:T(128)S(1)} %copy-done.13, s32[3,32768]{1,0:T(4,128)S(1)} %copy-done.6, s32[3,32768]{1,0:T(4,128)S(1)} %copy-done.8, bf16[128,48,256]{2,1,0:T(8,128)(2,1)S(1)} %bitcast.9), custom_call_target="tpu_custom_call" | custom-call | flops 2415919104 | bytes 7340032 | tf_op jit(solution)/shard_map/sample/pallas_call | solution.py:624
  176.8 0.0 copy-done.14
  176.8 0.4 reshape.32
  177.2 1.3 copy.13
Async XLA Ops:
  2.4 1.6 copy-start.3
  4.0 1.0 copy-start.4
  5.0 1.0 copy-start.5
  6.0 1.0 copy-start.7
  7.1 0.9 copy-start.9
  8.0 0.7 copy-start.10
  8.6 0.7 copy-start.11
  9.3 0.7 copy-start.12
  32.9 2.0 %copy-start = (bf16[128,64,256]{2,1,0:T(8,128)(2,1)}, bf16[128,64,256]{2,1,0:T(8,128)(2,1)S(1)}, u32[]{:S(2)}) copy-start(bf16[128,64,256]{2,1,0:T(8,128)(2,1)S(1)} %get-tuple-element.10) | copy-start | bytes 12582916
  34.9 0.6 copy-start.1
  35.5 121.6 %copy-start.6 = (s32[3,32768]{1,0:T(4,128)S(1)}, s32[3,32768]{1,0:T(4,128)}, u32[]{:S(2)}) copy-start(s32[3,32768]{1,0:T(4,128)} %cell_ref.3) | copy-start | bytes 1179652
  35.5 121.6 %copy-start.8 = (s32[3,32768]{1,0:T(4,128)S(1)}, s32[3,32768]{1,0:T(4,128)}, u32[]{:S(2)}) copy-start(s32[3,32768]{1,0:T(4,128)} %fraction_ref.3) | copy-start | bytes 1179652
  35.5 121.6 %copy-start.13 = (s32[64]{0:T(128)S(1)}, s32[64]{0:T(128)}, u32[]{:S(2)}) copy-start(s32[64]{0:T(128)} %count_ref.3) | copy-start | bytes 772
  157.1 1.9 %copy-start.2 = (bf16[4,8,4,48,256]{4,3,2,1,0:T(8,128)(2,1)S(1)}, bf16[4,8,4,48,256]{4,3,2,1,0:T(8,128)(2,1)}, u32[]{:S(2)}) copy-start(bf16[4,8,4,48,256]{4,3,2,1,0:T(8,128)(2,1)} %get-tuple-element.14) | copy-start | bytes 9437188
  159.0 17.8 %copy-start.14 = (f32[16,48,256]{2,1,0:T(8,128)S(1)}, f32[16,48,256]{2,1,0:T(8,128)}, u32[]{:S(2)}) copy-start(f32[16,48,256]{2,1,0:T(8,128)} %get-tuple-element.12) | copy-start | bytes 2359300

commit v3 on v2

v3 whole, which is shorter than its diff:
```python
import jax
import jax.numpy as jnp
from jax import lax
from jax.experimental import pallas as pl
from jax.experimental.pallas import tpu as pltpu
from jax.sharding import PartitionSpec as P

EDGE = 16
QUANT = 1024
PLANE = EDGE * EDGE
LANES = 128
CHUNK = 4
MESH = pl.DeviceIdType.MESH
ORDER = ((4, None, 0), (3, 0, 1), (-3, 1, 1), (2, 0, 2), (-2, 1, 2), (1, 0, 3), (-1, 1, 3), (0, None, 4))


def stencil(cell, fraction):
    position = cell.astype(jnp.float32) + 0.5 + (fraction.astype(jnp.float32) + 0.5) / QUANT
    node = lax.broadcasted_iota(jnp.int32, (EDGE, position.shape[1]), 0).astype(jnp.float32)
    offset = node - position
    magnitude = jnp.abs(offset)
    inner = 0.75 - magnitude * magnitude
    reach = jnp.maximum(1.5 - magnitude, 0.0)
    weight = jnp.where(magnitude < 0.5, inner, 0.5 * reach * reach)
    return weight, weight * offset


def fill_planes(cell_ref, fraction_ref, columns, rows_ref, plane_ref):
    width = rows_ref.shape[1]
    weight_y, slope_y = stencil(cell_ref[1:2, columns], fraction_ref[1:2, columns])
    weight_z, slope_z = stencil(cell_ref[2:3, columns], fraction_ref[2:3, columns])
    rows_ref[0:EDGE, :] = weight_y
    rows_ref[EDGE : 2 * EDGE, :] = slope_y
    for y in range(EDGE):
        rows = slice(y * EDGE, (y + 1) * EDGE)
        along = rows_ref[y : y + 1, :]
        tilt = rows_ref[EDGE + y : EDGE + y + 1, :]
        plane_ref[rows, 0:width] = (along * weight_z).astype(jnp.bfloat16)
        plane_ref[rows, width : 2 * width] = (tilt * weight_z).astype(jnp.bfloat16)
        plane_ref[rows, 2 * width : 3 * width] = (along * slope_z).astype(jnp.bfloat16)


def plan_kernel(
    owner_ref,
    slot_ref,
    count_ref,
    block_ref,
    place_ref,
    row_ref,
    filled_ref,
    source_ref,
    names_ref,
    stages_ref,
    used_ref,
    raw_ref,
    *,
    ring,
    side,
    capacity,
):
    blocks = owner_ref.shape[0]
    slots = ring * side * capacity
    g = lax.axis_index("gy")
    names_ref[...] = jnp.full_like(names_ref, -1.0)
    for key in range(ring * side):
        used_ref[key] = 0
    for slot in range(slots):
        raw_ref[slot] = -1

    @pl.loop(0, blocks)
    def _(block):
        owner = owner_ref[block]
        column, tall = lax.rem(owner, side), lax.div(owner, side)
        ahead = lax.rem(tall - g + ring, ring)
        distance = jnp.minimum(ahead, ring - ahead)
        stage = ring - 2 * distance - jnp.where(ahead < ring // 2, 1, 0)
        key = stage * side + column
        rank = used_ref[key]
        used_ref[key] = rank + 1
        raw_ref[key * capacity + rank] = block
        name = lax.convert_element_type(slot_ref[block], jnp.float32)
        line = (column * ring + stage) * capacity + rank
        names_ref[pl.ds(line, 1), :] = jnp.full((1, LANES), name, jnp.float32)

    def sweep(slot, found):
        block = raw_ref[slot]
        here = block >= 0
        block = jnp.maximum(block, 0)
        source_ref[slot] = jnp.where(here, found, 0)
        block_ref[found] = block
        filled_ref[found] = count_ref[block]
        row_ref[found] = lax.rem(slot, side * capacity)
        place_ref[jnp.where(here, block, blocks)] = found
        stage = lax.convert_element_type(lax.div(slot, side * capacity), jnp.float32)
        stages_ref[pl.ds(found, 1), :] = jnp.full((1, LANES), stage, jnp.float32)
        return found + jnp.where(here, 1, 0)

    lax.fori_loop(0, slots, sweep, 0)


def make_plan(owner, slot, count, ring, side, capacity):
    blocks = owner.shape[0]
    slots = ring * side * capacity
    scalars = pl.BlockSpec(memory_space=pltpu.SMEM)
    listed = jax.ShapeDtypeStruct((blocks + 8,), jnp.int32)

    def kernel(*refs):
        plan_kernel(*refs, ring=ring, side=side, capacity=capacity)

    return pl.pallas_call(
        kernel,
        in_specs=[scalars] * 3,
        out_specs=[scalars] * 5 + [pl.BlockSpec(memory_space=pltpu.VMEM)] * 2,
        out_shape=[listed] * 4
        + [
            jax.ShapeDtypeStruct((slots,), jnp.int32),
            jax.ShapeDtypeStruct((slots, LANES), jnp.float32),
            jax.ShapeDtypeStruct((blocks + 8, LANES), jnp.float32),
        ],
        scratch_shapes=[pltpu.SMEM((ring * side,), jnp.int32), pltpu.SMEM((slots,), jnp.int32)],
        name="plan",
    )(owner, slot, count)


def transfer_kernel(
    block_ref,
    place_ref,
    row_ref,
    filled_ref,
    source_ref,
    names_ref,
    stages_ref,
    mass_hbm,
    motion_hbm,
    affine_hbm,
    cell_hbm,
    fraction_hbm,
    drag_hbm,
    velocity_ref,
    new_velocity_ref,
    new_affine_ref,
    mass_ref,
    motion_ref,
    affine_ref,
    cell_ref,
    fraction_ref,
    drag_ref,
    packed,
    slots_out,
    slot_in,
    name_in,
    relay,
    part_out,
    part_in,
    own_names,
    table,
    own_sum,
    grid_all,
    reply,
    relay_back,
    rows_ref,
    plane_ref,
    lead_ref,
    found_velocity,
    found_affine,
    load_sem,
    name_send,
    name_recv,
    out_send,
    out_recv,
    part_send,
    part_recv,
    grid_send,
    grid_recv,
    back_send,
    back_recv,
    *back,
):
    ring, side, capacity = slots_out.shape[:3]
    tiles = drag_ref.shape[0]
    chunks = tiles // CHUNK
    half = capacity // 2
    steps = ring // 2
    blocks = packed.shape[0]
    batch = side * capacity
    width = rows_ref.shape[2]
    g, q = lax.axis_index("gy"), lax.axis_index("gz")
    q_up, q_down, q_far = lax.rem(q + 1, side), lax.rem(q + side - 1, side), lax.rem(q + 2, side)
    up, down, far = {"gz": q_up}, {"gz": q_down}, {"gz": q_far}
    along = ({"gy": lax.rem(g + 1, ring)}, {"gy": lax.rem(g + ring - 1, ring)})
    owners = [lax.rem(g + delta + ring, ring) for delta, _, _ in ORDER]

    loads = [
        pltpu.make_async_copy(source, target, load_sem.at[k])
        for k, (source, target) in enumerate(
            (
                (cell_hbm, cell_ref),
                (fraction_hbm, fraction_ref),
                (mass_hbm, mass_ref),
                (motion_hbm, motion_ref),
                (affine_hbm, affine_ref),
                (drag_hbm, drag_ref),
            )
        )
    ]
    for item in loads:
        item.start()

    def copy(source, target, send, recv, device):
        return pltpu.make_async_remote_copy(
            src_ref=source,
            dst_ref=target,
            send_sem=send,
            recv_sem=recv,
            device_id=device,
            device_id_type=MESH,
        )

    barrier = pltpu.get_barrier_semaphore()
    peers = (up, down, far) + along
    for peer in peers:
        pl.semaphore_signal(barrier, inc=1, device_id=peer, device_id_type=MESH)
    lead_ref[...] = jnp.zeros_like(lead_ref)
    for item in loads:
        item.wait()

    def deposit(k, part):
        block = block_ref[k]
        columns = pl.ds(block * width, width)
        plane, lead = plane_ref.at[part], lead_ref.at[part]
        fill_planes(cell_ref, fraction_ref, columns, rows_ref.at[part], plane)
        weight, slope = stencil(cell_ref[0:1, columns], fraction_ref[0:1, columns])
        lane = lax.broadcasted_iota(jnp.int32, (1, width), 1)
        mass = jnp.where(lane < filled_ref[k], mass_ref[0:1, columns], 0.0)
        lead[0:EDGE, 0:width] = (mass * weight).astype(jnp.bfloat16)
        for d in range(3):
            rows = slice((d + 1) * EDGE, (d + 2) * EDGE)
            motion = motion_ref[d : d + 1, columns]
            first = affine_ref[3 * d : 3 * d + 1, columns]
            second = mass * affine_ref[3 * d + 1 : 3 * d + 2, columns]
            third = mass * affine_ref[3 * d + 2 : 3 * d + 3, columns]
            lead[rows, 0:width] = (mass * (motion * weight + first * slope)).astype(jnp.bfloat16)
            lead[rows, width : 2 * width] = (second * weight).astype(jnp.bfloat16)
            lead[rows, 2 * width : 3 * width] = (third * weight).astype(jnp.bfloat16)
        total = lax.dot_general(
            lead[...], plane[...], (((1,), (1,)), ((), ())), preferred_element_type=jnp.float32
        )
        packed[k] = total.astype(jnp.bfloat16)

    def deposit_batch(b):
        @pl.loop(0, batch // 2)
        def _(pair):
            deposit(b * batch + 2 * pair, 0)
            deposit(b * batch + 2 * pair + 1, 1)

    def spread(row, count):
        factor = jnp.broadcast_to(row, (EDGE, LANES)).astype(jnp.bfloat16)
        factor = jnp.concatenate([factor, factor], axis=1)
        return jnp.concatenate([factor] * count, axis=0)

    def assemble(i):
        for column in range(side):

            @pl.loop(0, capacity)
            def _(r):
                place = source_ref[(i * side + column) * capacity + r]
                name = names_ref[column, pl.ds(i * capacity + r, 1), :]
                slots_out[i, column, r] = packed[place] * spread(jnp.where(name >= 0.0, 1.0, 0.0), 4)

    name_copies = [
        copy(names_ref.at[there], name_in.at[k], name_send.at[k], name_recv.at[k], device)
        for k, (there, device) in enumerate(((q_up, up), (q_down, down), (q_far, far)))
    ]

    def outward(i):
        return [
            copy(slots_out.at[i, q_up], slot_in.at[0, i], out_send.at[i, 0], out_recv.at[i, 0], up),
            copy(slots_out.at[i, q_down], slot_in.at[1, i], out_send.at[i, 1], out_recv.at[i, 1], down),
            copy(
                slots_out.at[i, q_far, pl.ds(0, half)],
                relay.at[0, i],
                out_send.at[i, 2],
                out_recv.at[i, 2],
                up,
            ),
            copy(
                slots_out.at[i, q_far, pl.ds(half, half)],
                relay.at[1, i],
                out_send.at[i, 3],
                out_recv.at[i, 3],
                down,
            ),
            copy(
                relay.at[0, i],
                slot_in.at[2, i, pl.ds(0, half)],
                out_send.at[i, 4],
                out_recv.at[i, 4],
                up,
            ),
            copy(
                relay.at[1, i],
                slot_in.at[2, i, pl.ds(half, half)],
                out_send.at[i, 5],
                out_recv.at[i, 5],
                down,
            ),
        ]

    out = [outward(i) for i in range(ring)]

    def first_hop(i):
        if i < ring:
            for k in (2, 3, 0, 1):
                out[i][k].start()

    def second_hop(i):
        if i < ring:
            for k in (0, 1):
                out[i][2 + k].wait_recv()
                out[i][4 + k].start()

    def part_copy(way, e, c):
        rows = pl.ds(c * CHUNK, CHUNK)
        return copy(
            part_out.at[way, e, rows],
            part_in.at[way, e, rows],
            part_send.at[way, e, c],
            part_recv.at[way, e, c],
            along[way],
        )

    def prepare(i):
        for role in range(4):
            source = names_ref.at[q] if role == 3 else name_in.at[role]
            lines = slice(role * capacity, (role + 1) * capacity)
            own_names[lines, :] = source[i * capacity : (i + 1) * capacity, :]
        named = own_names[...]
        for t in range(tiles):
            table[i, t] = jnp.where(named == float(t), 1.0, 0.0)

    def add_up(i, c, incoming, put):
        @pl.loop(0, 4)
        def _(d):
            rows = pl.ds(pl.multiple_of(d * EDGE, EDGE), EDGE)
            sums = [None] * CHUNK
            for role in range(4):
                for r in range(capacity):
                    source = slots_out.at[i, q, r] if role == 3 else slot_in.at[role, i, r]
                    value = source[rows, :].astype(jnp.float32)
                    line = role * capacity + r
                    for t in range(CHUNK):
                        factor = table[i, c * CHUNK + t, line : line + 1, :]
                        term = jnp.concatenate([factor, factor], axis=1) * value
                        sums[t] = term if sums[t] is None else sums[t] + term
            for t in range(CHUNK):
                total = sums[t]
                for way, e in incoming:
                    total = total + part_in[way, e, c * CHUNK + t, rows, :].astype(jnp.float32)
                put(c, t, rows, total)

    def send_parts(i, way, e, first, last, incoming):
        @pl.loop(first, last)
        def _(k):
            c = lax.rem(k + way * (chunks // 2), chunks)
            for w, before in incoming:
                part_copy(w, before, c).wait_recv()

            def put(c, t, rows, total):
                part_out[way, e, c * CHUNK + t, rows, :] = total.astype(jnp.bfloat16)

            add_up(i, c, incoming, put)
            part_copy(way, e, c).start()

    def gather(i):
        _, way, e = ORDER[i]
        prepare(i)
        for k in (0, 1, 4, 5):
            out[i][k].wait_recv()
        if e == 0:
            send_parts(i, 0, 0, 0, chunks // 2, ())
            send_parts(i, 1, 0, 0, chunks // 2, ())
        elif e == 1:
            send_parts(i, way, e, 0, chunks // 2, ((way, 0),))
            send_parts(i, way, e, chunks // 2, chunks, ())
        elif e < steps:
            send_parts(i, way, e, 0, chunks, ((way, e - 1),))

    deposit_batch(0)
    assemble(0)
    pl.semaphore_wait(barrier, len(peers))
    for item in name_copies:
        item.start()
    first_hop(0)
    deposit_batch(1)
    assemble(1)
    second_hop(0)
    first_hop(1)
    for item in name_copies:
        item.wait_recv()
    deposit_batch(2)
    assemble(2)
    second_hop(1)
    first_hop(2)
    gather(0)
    deposit_batch(3)
    for i in range(3, ring):
        assemble(i)
    first_hop(3)
    for i in range(1, ring):
        second_hop(i + 1)
        first_hop(i + 3)
        gather(i)

    def grid_copy(way, e, c):
        o = lax.rem(g + (ring - e if way == 0 else e), ring)
        rows = pl.ds(c * CHUNK, CHUNK)
        return copy(
            grid_all.at[o, rows],
            grid_all.at[o, rows],
            grid_send.at[way, e, c],
            grid_recv.at[way, e, c],
            along[way],
        )

    @pl.loop(0, chunks)
    def _(c):
        for way in (0, 1):
            part_copy(way, steps - 1, c).wait_recv()

        def put(c, t, rows, total):
            own_sum[t, rows, :] = total

        add_up(ring - 1, c, ((0, steps - 1), (1, steps - 1)), put)
        for t in range(CHUNK):
            tile = c * CHUNK + t
            mass = own_sum[t, 0:EDGE, :] + drag_ref[tile]
            for d in range(3):
                rows = slice(d * EDGE, (d + 1) * EDGE)
                value = own_sum[t, (d + 1) * EDGE : (d + 2) * EDGE, :] / mass
                velocity_ref[tile, rows, :] = value
                grid_all[g, tile, rows, :] = value.astype(jnp.bfloat16)
        for way in (0, 1):
            grid_copy(way, 0, c).start()

    def inward(i):
        mine = pl.ds(q * capacity, capacity)
        return [
            copy(reply.at[1, i], back[i].at[mine], back_send.at[i, 0], back_recv.at[i, 0], up),
            copy(reply.at[0, i], back[i].at[mine], back_send.at[i, 1], back_recv.at[i, 1], down),
            copy(
                reply.at[2, i, pl.ds(0, half)],
                relay_back.at[0, i],
                back_send.at[i, 2],
                back_recv.at[i, 2],
                up,
            ),
            copy(
                reply.at[2, i, pl.ds(half, half)],
                relay_back.at[1, i],
                back_send.at[i, 3],
                back_recv.at[i, 3],
                down,
            ),
            copy(
                relay_back.at[0, i],
                back[i].at[pl.ds(q_down * capacity, half)],
                back_send.at[i, 4],
                back_recv.at[i, 4],
                up,
            ),
            copy(
                relay_back.at[1, i],
                back[i].at[pl.ds(q_up * capacity + half, half)],
                back_send.at[i, 5],
                back_recv.at[i, 5],
                down,
            ),
        ]

    replies = [inward(i) for i in range(ring)]

    def pick(i, role, r, target):
        o = owners[i]
        line = role * capacity + r
        total = None
        for t in range(tiles):
            term = spread(table[i, t, pl.ds(line, 1), :], 3) * grid_all[o, t]
            total = term if total is None else total + term
        target[...] = total

    def answer(i):
        @pl.loop(0, capacity)
        def _(r):
            for role in range(3):
                pick(i, role, r, reply.at[role, i, r])
            pick(i, 3, r, back[i].at[q * capacity + r])

        for k in (2, 3, 0, 1):
            replies[i][k].start()

    def pass_back(i):
        for k in (0, 1):
            replies[i][2 + k].wait_recv()
            replies[i][4 + k].start()

    def arrived(i):
        for k in (0, 1, 4, 5):
            replies[i][k].wait_recv()

    def sample(k, part, first):
        block = block_ref[k]
        stage, row = stages_ref[pl.ds(k, 1), :], row_ref[k]
        columns = pl.ds(block * width, width)
        plane = plane_ref.at[part]
        fill_planes(cell_ref, fraction_ref, columns, rows_ref.at[part], plane)
        weight, slope = stencil(cell_ref[0:1, columns], fraction_ref[0:1, columns])
        nodes = None
        for i in range(first, ring):
            term = spread(jnp.where(stage == float(i), 1.0, 0.0), 3) * back[i][row]
            nodes = term if nodes is None else nodes + term
        moments = jnp.dot(nodes, plane[...], preferred_element_type=jnp.float32)
        lane = lax.broadcasted_iota(jnp.int32, (1, width), 1)
        present = lane < filled_ref[k]

        def reduced(d, which, factor):
            moment = moments[d * EDGE : (d + 1) * EDGE, which * width : (which + 1) * width]
            total = jnp.sum(factor * moment, axis=0, keepdims=True)
            return jnp.where(present, total, 0.0)

        for d in range(3):
            found_velocity[k, d : d + 1, :] = reduced(d, 0, weight)
            found_affine[k, 3 * d : 3 * d + 1, :] = 4.0 * reduced(d, 0, slope)
            found_affine[k, 3 * d + 1 : 3 * d + 2, :] = 4.0 * reduced(d, 1, weight)
            found_affine[k, 3 * d + 2 : 3 * d + 3, :] = 4.0 * reduced(d, 2, weight)

    def sample_batch(b):
        @pl.loop(0, batch // 2)
        def _(pair):
            sample(b * batch + 2 * pair, 0, b)
            sample(b * batch + 2 * pair + 1, 1, b)

    def take(e, first, last, onward):
        @pl.loop(first, last)
        def _(k):
            for way in (0, 1):
                c = lax.rem(k + way * (chunks // 2), chunks)
                grid_copy(way, e, c).wait_recv()
                if onward:
                    grid_copy(way, e + 1, c).start()

    answer(7)
    take(0, 0, chunks // 2, True)
    pass_back(7)
    take(0, chunks // 2, chunks, True)
    answer(6)
    answer(5)
    take(1, 0, chunks // 2, True)
    pass_back(6)
    pass_back(5)
    take(1, chunks // 2, chunks, True)
    answer(4)
    answer(3)
    take(2, 0, chunks // 2, True)
    pass_back(4)
    pass_back(3)
    take(2, chunks // 2, chunks, False)
    answer(2)
    answer(1)
    for i in (7, 6, 5, 4, 3):
        arrived(i)
    sample_batch(3)
    take(3, 0, chunks // 2, False)
    answer(0)
    pass_back(2)
    pass_back(1)
    pass_back(0)
    arrived(2)
    sample_batch(2)
    arrived(1)
    sample_batch(1)
    arrived(0)
    sample_batch(0)

    @pl.loop(0, blocks)
    def _(block):
        columns = pl.ds(pl.multiple_of(block * width, width), width)
        place = place_ref[block]
        new_velocity_ref[:, columns] = found_velocity[place]
        new_affine_ref[:, columns] = found_affine[place]

    for item in name_copies:
        item.wait_send()
    for i in range(ring):
        for k in range(6):
            out[i][k].wait_send()
            replies[i][k].wait_send()
    for way in (0, 1):
        for e in range(1, steps):

            @pl.loop(0, chunks)
            def _(c):
                part_copy(way, e, c).wait_send()
                grid_copy(way, e - 1, c).wait_send()

        @pl.loop(0, chunks // 2)
        def _(k):
            c = k + way * (chunks // 2)
            part_copy(way, 0, c).wait_send()
            grid_copy(way, steps - 1, c).wait_send()


def transfer(plan, blocks, mass, motion, affine, cell, fraction, drag, ring, side, capacity):
    total = cell.shape[1]
    width = total // blocks
    tiles = drag.shape[0]
    steps = ring // 2
    chunks = tiles // CHUNK
    half = capacity // 2
    scalars = pl.BlockSpec(memory_space=pltpu.SMEM)
    whole = pl.BlockSpec(memory_space=pltpu.VMEM)
    outside = pl.BlockSpec(memory_space=pltpu.HBM)
    dma = pltpu.SemaphoreType.DMA
    block, answer = (4 * EDGE, PLANE), (3 * EDGE, PLANE)
    *lists, names, stages = plan
    return pl.pallas_call(
        transfer_kernel,
        in_specs=[scalars] * 5 + [whole] * 2 + [outside] * 6,
        out_specs=[whole] * 3,
        out_shape=[
            jax.ShapeDtypeStruct((tiles,) + answer, jnp.float32),
            jax.ShapeDtypeStruct((3, total), jnp.float32),
            jax.ShapeDtypeStruct((9, total), jnp.float32),
        ],
        scratch_shapes=[
            pltpu.VMEM((1, total), jnp.float32),
            pltpu.VMEM((3, total), jnp.float32),
            pltpu.VMEM((9, total), jnp.float32),
            pltpu.VMEM((3, total), jnp.int32),
            pltpu.VMEM((3, total), jnp.int32),
            pltpu.VMEM(drag.shape, jnp.float32),
            pltpu.VMEM((blocks,) + block, jnp.bfloat16),
            pltpu.VMEM((ring, side, capacity) + block, jnp.bfloat16),
            pltpu.VMEM((3, ring, capacity) + block, jnp.bfloat16),
            pltpu.VMEM((3, ring * capacity, LANES), jnp.float32),
            pltpu.VMEM((2, ring, half) + block, jnp.bfloat16),
            pltpu.VMEM((2, steps, tiles) + block, jnp.bfloat16),
            pltpu.VMEM((2, steps, tiles) + block, jnp.bfloat16),
            pltpu.VMEM((4 * capacity, LANES), jnp.float32),
            pltpu.VMEM((ring, tiles, 4 * capacity, LANES), jnp.float32),
            pltpu.VMEM((CHUNK,) + block, jnp.float32),
            pltpu.VMEM((ring, tiles) + answer, jnp.bfloat16),
            pltpu.VMEM((3, ring, capacity) + answer, jnp.bfloat16),
            pltpu.VMEM((2, ring, half) + answer, jnp.bfloat16),
            pltpu.VMEM((2, 2 * EDGE, width), jnp.float32),
            pltpu.VMEM((2, PLANE, 3 * width), jnp.bfloat16),
            pltpu.VMEM((2, 4 * EDGE, 3 * width), jnp.bfloat16),
            pltpu.VMEM((blocks, 3, width), jnp.float32),
            pltpu.VMEM((blocks, 9, width), jnp.float32),
            dma((6,)),
            dma((3,)),
            dma((3,)),
            dma((ring, 6)),
            dma((ring, 6)),
            dma((2, steps, chunks)),
            dma((2, steps, chunks)),
            dma((2, steps, chunks)),
            dma((2, steps, chunks)),
            dma((ring, 6)),
            dma((ring, 6)),
        ]
        + [pltpu.VMEM((side * capacity,) + answer, jnp.bfloat16)] * ring,
        compiler_params=pltpu.CompilerParams(
            collective_id=0, has_side_effects=True, vmem_limit_bytes=62 << 20
        ),
        cost_estimate=pl.CostEstimate(flops=1 << 32, bytes_accessed=8 << 20, transcendentals=0),
        name="transfer",
    )(
        *lists,
        names.reshape(side, ring * capacity, LANES),
        stages,
        mass.reshape(1, -1),
        motion,
        affine,
        cell,
        fraction,
        drag,
    )


def per_device(
    particle_mass,
    particle_velocity,
    particle_affine,
    particle_cell,
    particle_fraction,
    block_owner,
    block_slot,
    block_count,
    cell_drag,
):
    ring, side = lax.axis_size("gy"), lax.axis_size("gz")
    blocks = block_count.shape[0]
    capacity = max(1, 2 * blocks // (ring * side))
    tiles = cell_drag.shape[0]
    plan = make_plan(block_owner.reshape(-1), block_slot, block_count, ring, side, capacity)
    velocity, new_velocity, new_affine = transfer(
        plan,
        blocks,
        particle_mass,
        particle_velocity,
        particle_affine,
        particle_cell,
        particle_fraction,
        cell_drag.reshape(tiles, EDGE, PLANE),
        ring,
        side,
        capacity,
    )
    return (velocity.reshape(tiles, 3, -1), new_velocity, new_affine)


def solution(mesh):
    split = ("gx", "gy", "gz")
    return jax.shard_map(
        per_device,
        mesh=mesh,
        in_specs=(
            P(split),
            P(None, split),
            P(None, split),
            P(None, split),
            P(None, split),
            P(split, None),
            P(split),
            P(split),
            P(split, None),
        ),
        out_specs=(P(split, None, None), P(None, split), P(None, split)),
        check_vma=False,
    )
```

time: 179 us -> 146 us (0.82)
  the two profiles are of different devices: /device:TPU:4 before, /device:TPU:34 now
where the time goes in v3:
time: 146 us
  Pallas kernels  138 us (95%)
  local copies, waits for them, and re-layouts  6.88 us (5%)
    pallas_call x1, Pallas kernels, transfer(): pl.pallas_call(transfer_kernel, in_specs=[scalars] * 5 + [whole] * 2 + [o...  133 us
    unnamed x8, local copies, waits for them, and re-layouts  5.2 us
    pallas_call x1, Pallas kernels, make_plan(): pl.pallas_call(kernel, in_specs=[scalars] * 3, out_specs=[scalars] * 5 +...  4.68 us

profile of v3, /device:TPU:34, one launch (start us, length us, event | category | flops | bytes accessed | tf_op | source)
XLA Modules:
  0.0 145.7 jit_solution(16949341147391611421)
XLA Ops:
  0.6 4.7 %plan.1 = (s32[72]{0:T(128)}, s32[72]{0:T(128)}, s32[72]{0:T(128)}, s32[72]{0:T(128)}, s32[128]{0:T(128)}, /*index=5*/f32[128,128]{1,0:T(8,128)}, f32[72,128]{1,0:T(8,128)}) custom-call(s32[64]{0:T(128)} %bitcast.8, s32[64]{0:T(128)} %refs_1_.1, s32[64]{0:T(128)} %refs_2_.1), custom_call_target="tpu_custom_call" | custom-call | tf_op jit(solution)/shard_map/plan/pallas_call | solution.py:110
  5.3 1.7 %copy.14 = f32[2,8,16,256]{3,2,1,0:T(8,128)} copy(f32[2,8,16,256]{3,1,2,0:T(8,128)} %bitcast.5) | data formatting | bytes 524288
  7.1 133.5 %transfer.1 = (f32[16,48,256]{2,1,0:T(8,128)}, f32[3,32768]{1,0:T(4,128)}, f32[9,32768]{1,0:T(8,128)}) custom-call(s32[72]{0:T(128)} %get-tuple-element.13.block_ref, s32[72]{0:T(128)} %get-tuple-element.14.place_ref, s32[72]{0:T(128)} %get-tuple-element.15.row_ref, s32[72]{0:T(128)} %get-tuple-element.16.filled_ref, s32[128]{0:T(128)} %get-tuple-element.17.source_ref, ...), custom_call_target="tpu_custom_call" | custom-call | flops 4294967296 | bytes 8388608 | tf_op jit(solution)/shard_map/transfer/pallas_call | solution.py:625
  140.5 0.0 copy-start
  140.5 1.7 %reshape.25 = f32[16,3,4096]{2,1,0:T(4,128)S(1)} reshape(f32[16,48,256]{2,1,0:T(8,128)} %get-tuple-element.20) | data formatting | bytes 1572864 | tf_op jit(solution)/shard_map/reshape | solution.py:719
  142.2 0.0 copy-start.1
  142.2 1.3 copy.13
  143.6 0.0 copy-done.1
  143.6 0.8 copy.17
  144.4 0.0 copy-done
  144.4 1.3 copy.18
Async XLA Ops:
  140.5 3.8 %copy-start = (f32[9,32768]{1,0:T(8,128)S(1)}, f32[9,32768]{1,0:T(8,128)}, u32[]{:S(2)}) copy-start(f32[9,32768]{1,0:T(8,128)} %get-tuple-element.34) | copy-start | bytes 3538948
  142.2 1.4 copy-start.1
